TPU v7x, 32 devices: a whole 2x2x4 slice. The times are simulated.
32 devices in a mesh: replica: 8 (over z, x), tensor: 4 (over y, core).
Axes of the slice: x: 2, y: 2, z: 4, core: 2. Of those that a mesh axis runs over, the one named last changes fastest.
Arguments:
- queries: bfloat16 [512, 8192], P('replica', 'tensor'), may hold values from -18 to 18
- kv_new: bfloat16 [512, 2, 1024], P('replica', None, 'tensor'), may hold values from -7.5 to 7.5
- pool: bfloat16 [192, 128, 2, 1024], P('replica', None, None, 'tensor'), may hold values from -240 to 240
- page_table: int32 [16, 12], P('replica'), may hold values from 0 to 191, as said below
- hist_len: int32 [16], P('replica'), may hold values from 769 to 1536
- o_weight: bfloat16 [8192, 8192], P('tensor'), may hold values from -0.125 to 0.125
Outputs:
- mixed: bfloat16 [512, 8192], P(('replica', 'tensor'))
Inputs may be any that keep to these rules, and one draw needn't show every extreme that they name: `page_table`: no two entries are equal. The owner of page id g is the replica group g // 24. Among the live pages (entry j of conversation c with j * 128 < hist_len[c]) of the conversations of one replica group, at most 3 have any one owner, and in every group some owner holds exactly 3 of them.
All inputs are finite; a program needn't handle non-finite values.
Results may differ from a plain program's by a relative error of at most 0.014.
Values may be sent and summed in bfloat16 or wider, within the bound.
A program may use at most 128 MiB of HBM per device.

v0:
```python
import functools
import math

import jax
import jax.numpy as jnp
from jax import lax
from jax.experimental import pallas as pl
from jax.experimental.pallas import tpu as pltpu
from jax.sharding import PartitionSpec as P

HD = 128
PAGE = 128
SLOT = 3
TILE = 1024


floor_value = -1e30

MESH = pl.DeviceIdType.MESH


def kernel(
    groups, shards, new_len,
    shelf_ref, dialog_ref, fill_ref, q_ref, fresh_ref, pool_ref, weight,
    out_ref,
    outgoing, arrived, wbuf, perm, qs, kbuf, vbuf, peak_ref, amount_ref, summed_ref, attended, part, landed,
    send_sem, recv_sem, weight_sem, part_send, part_recv,
):
    me = lax.axis_index("replica")
    mine = lax.axis_index("tensor")
    token_rows = q_ref.shape[0]
    kv_count, rows, _ = qs.shape
    per_group = rows // token_rows
    slots = arrived.shape[1]
    tiles, _, block_rows, tile = part.shape
    scale = 1.0 / math.sqrt(HD)

    barrier = pltpu.get_barrier_semaphore()
    for step in range(1, groups):
        pl.semaphore_signal(
            barrier, inc=1, device_id={"replica": lax.rem(me + step, groups)}, device_id_type=MESH
        )
    for step in range(1, shards):
        pl.semaphore_signal(
            barrier, inc=1, device_id={"tensor": lax.rem(mine + step, shards)}, device_id_type=MESH
        )

    def collect(step, carry):
        dest = lax.rem(me + step, groups)
        for s in range(slots):
            outgoing[step, s] = pool_ref[shelf_ref[dest, s]]
        return carry

    lax.fori_loop(0, groups, collect, 0)
    pl.semaphore_wait(barrier, groups + shards - 2)

    def page_copy(step):
        dest = lax.rem(me + step, groups)
        return pltpu.make_async_remote_copy(
            src_ref=outgoing.at[step],
            dst_ref=arrived.at[step],
            send_sem=send_sem.at[step],
            recv_sem=recv_sem.at[step],
            device_id={"replica": dest},
            device_id_type=MESH,
        )

    def weight_copy(index):
        return pltpu.make_async_copy(
            weight.at[:, pl.ds(pl.multiple_of(index * tile, tile), tile)],
            wbuf.at[index],
            weight_sem.at[index],
        )

    def part_copy(index, step):
        dest = lax.rem(mine + step, shards)
        return pltpu.make_async_remote_copy(
            src_ref=part.at[index, dest],
            dst_ref=landed.at[index, step - 1],
            send_sem=part_send.at[index, step - 1],
            recv_sem=part_recv.at[index, step - 1],
            device_id={"tensor": dest},
            device_id_type=MESH,
        )

    for step in range(1, groups):
        page_copy(step).start()
    for index in range(tiles):
        weight_copy(index).start()

    width = perm.shape[0]
    i = lax.broadcasted_iota(jnp.int32, (width, width), 0)
    j = lax.broadcasted_iota(jnp.int32, (width, width), 1)
    source = jnp.where(i < PAGE, 2 * i, 2 * (i - PAGE) + 1)
    perm[...] = jnp.where(source == j, 1.0, 0.0).astype(perm.dtype)

    for k in range(kv_count):
        for g in range(per_group):
            col = (k * per_group + g) * HD
            qs[k, g * token_rows : (g + 1) * token_rows, :] = q_ref[:, col : col + HD]

    contract = (((1,), (1,)), ((), ()))

    row_token = lax.broadcasted_iota(jnp.int32, (rows, token_rows), 0) % token_rows
    col_token = lax.broadcasted_iota(jnp.int32, (rows, token_rows), 1)
    causal = (row_token // new_len == col_token // new_len) & (col_token <= row_token)
    for k in range(kv_count):
        keys = fresh_ref[0, :, k * HD : (k + 1) * HD]
        values = fresh_ref[1, :, k * HD : (k + 1) * HD]
        scores = lax.dot_general(qs[k], keys, contract, preferred_element_type=jnp.float32) * scale
        scores = jnp.where(causal, scores, floor_value)
        peak = jnp.max(scores, axis=-1, keepdims=True)
        weights = jnp.exp(scores - peak).astype(jnp.bfloat16)
        peak_ref[k] = jnp.broadcast_to(peak, (rows, HD))
        amount_ref[k] = jnp.broadcast_to(
            jnp.sum(weights.astype(jnp.float32), axis=-1, keepdims=True), (rows, HD)
        )
        summed_ref[k] = jnp.dot(weights, values, preferred_element_type=jnp.float32)

    def absorb(step, pages):
        owner = lax.rem(me - step + groups, groups)
        row_dialog = (
            lax.broadcasted_iota(jnp.int32, (rows, PAGE), 0) % token_rows
        ) // new_len
        position = lax.broadcasted_iota(jnp.int32, (rows, PAGE), 1)
        allowed = []
        for s in range(slots):
            split = jnp.dot(perm[...], pages[step, s], preferred_element_type=jnp.float32)
            split = split.astype(jnp.bfloat16)
            kbuf[s * PAGE : (s + 1) * PAGE, :] = split[:PAGE]
            vbuf[s * PAGE : (s + 1) * PAGE, :] = split[PAGE:]
            limit = jnp.where(row_dialog == dialog_ref[owner, s], fill_ref[owner, s], 0)
            allowed.append(position < limit)
        for k in range(kv_count):
            keys = kbuf[:, k * HD : (k + 1) * HD]
            values = vbuf[:, k * HD : (k + 1) * HD]
            scores = (
                lax.dot_general(qs[k], keys, contract, preferred_element_type=jnp.float32) * scale
            )
            pieces = [
                jnp.where(allowed[s], scores[:, s * PAGE : (s + 1) * PAGE], floor_value)
                for s in range(slots)
            ]
            high = functools.reduce(jnp.maximum, pieces)
            before = peak_ref[k]
            peak = jnp.maximum(before, jnp.max(high, axis=-1, keepdims=True))
            keep = jnp.exp(before - peak)
            weights = [jnp.exp(piece - peak).astype(jnp.bfloat16) for piece in pieces]
            added = functools.reduce(jnp.add, [w.astype(jnp.float32) for w in weights])
            peak_ref[k] = peak
            amount_ref[k] = keep * amount_ref[k] + jnp.sum(added, axis=-1, keepdims=True)
            summed_ref[k] = keep * summed_ref[k] + jnp.dot(
                jnp.concatenate(weights, axis=1), values, preferred_element_type=jnp.float32
            )

    absorb(0, outgoing)

    def page_step(step, carry):
        page_copy(step).wait_recv()
        absorb(step, arrived)
        return carry

    lax.fori_loop(1, groups, page_step, 0)

    for k in range(kv_count):
        for g in range(per_group):
            span = slice(g * token_rows, (g + 1) * token_rows)
            col = (k * per_group + g) * HD
            attended[:, col : col + HD] = (summed_ref[k, span] / amount_ref[k, span]).astype(
                jnp.bfloat16
            )

    def project(index, carry):
        weight_copy(index).wait()
        product = jnp.dot(attended[...], wbuf[index], preferred_element_type=jnp.float32)
        part[index] = product.astype(jnp.bfloat16).reshape(shards, block_rows, tile)
        for step in range(1, shards):
            part_copy(index, step).start()
        return carry

    lax.fori_loop(0, tiles, project, 0)

    def finish(index, carry):
        total = part[index, mine].astype(jnp.float32)
        for step in range(1, shards):
            part_copy(index, step).wait_recv()
            total = total + landed[index, step - 1].astype(jnp.float32)
        out_ref[:, pl.ds(pl.multiple_of(index * tile, tile), tile)] = total.astype(out_ref.dtype)
        return carry

    lax.fori_loop(0, tiles, finish, 0)

    def drain(index, carry):
        for step in range(1, shards):
            part_copy(index, step).wait_send()
        return carry

    lax.fori_loop(0, tiles, drain, 0)
    for step in range(1, groups):
        page_copy(step).wait_send()


def request_lists(page_table, hist_len, groups, pool_size):
    dialogs, entries = page_table.shape
    position = jnp.arange(entries, dtype=jnp.int32)
    fills = jnp.clip(hist_len[:, None] - position[None, :] * PAGE, 0, PAGE).reshape(-1)
    owners = (page_table // pool_size).reshape(-1)
    shelf = (page_table % pool_size).reshape(-1)
    dialog_of = jnp.repeat(jnp.arange(dialogs, dtype=jnp.int32), entries)
    hits = (owners[:, None] == jnp.arange(groups, dtype=jnp.int32)[None, :]) & (fills > 0)[:, None]
    ranks = jnp.cumsum(hits.astype(jnp.int32), axis=0) - 1
    places = hits.T[:, None, :] & (
        ranks.T[:, None, :] == jnp.arange(SLOT, dtype=jnp.int32)[None, :, None]
    )
    picked = places.astype(jnp.int32)
    wanted = jnp.sum(picked * shelf[None, None, :], axis=-1)
    dialog_ids = jnp.sum(picked * dialog_of[None, None, :], axis=-1)
    slot_fill = jnp.sum(picked * fills[None, None, :], axis=-1)
    return (wanted, dialog_ids, slot_fill)


def local(queries, kv_new, pool, page_table, hist_len, o_weight):
    groups = lax.axis_size("replica")
    shards = lax.axis_size("tensor")
    pool_size, page_len, _, kv_width = pool.shape
    dialogs = page_table.shape[0]
    token_rows = queries.shape[0]
    new_len = token_rows // dialogs
    kv_count = kv_width // HD
    per_group = queries.shape[1] // kv_width
    rows = per_group * token_rows
    depth, model = o_weight.shape
    tile = min(TILE, model)
    tiles = model // tile
    block_rows = token_rows // shards
    wanted, dialog_ids, slot_fill = request_lists(page_table, hist_len, groups, pool_size)
    shelf_ids = lax.all_to_all(wanted, "replica", split_axis=0, concat_axis=0, tiled=True)
    pages = pool.reshape(pool_size, 2 * page_len, kv_width)
    fresh = jnp.stack([kv_new[:, 0], kv_new[:, 1]])
    vmem = pl.BlockSpec(memory_space=pltpu.VMEM)
    smem = pl.BlockSpec(memory_space=pltpu.SMEM)
    anywhere = pl.BlockSpec(memory_space=pl.ANY)
    return pl.pallas_call(
        functools.partial(kernel, groups, shards, new_len),
        out_shape=jax.ShapeDtypeStruct((block_rows, model), jnp.bfloat16),
        in_specs=[smem, smem, smem, vmem, vmem, vmem, anywhere],
        out_specs=vmem,
        scratch_shapes=[
            pltpu.VMEM((groups, SLOT, 2 * page_len, kv_width), jnp.bfloat16),
            pltpu.VMEM((groups, SLOT, 2 * page_len, kv_width), jnp.bfloat16),
            pltpu.VMEM((tiles, depth, tile), jnp.bfloat16),
            pltpu.VMEM((2 * page_len, 2 * page_len), jnp.bfloat16),
            pltpu.VMEM((kv_count, rows, HD), jnp.bfloat16),
            pltpu.VMEM((SLOT * page_len, kv_width), jnp.bfloat16),
            pltpu.VMEM((SLOT * page_len, kv_width), jnp.bfloat16),
            pltpu.VMEM((kv_count, rows, HD), jnp.float32),
            pltpu.VMEM((kv_count, rows, HD), jnp.float32),
            pltpu.VMEM((kv_count, rows, HD), jnp.float32),
            pltpu.VMEM((token_rows, depth), jnp.bfloat16),
            pltpu.VMEM((tiles, shards, block_rows, tile), jnp.bfloat16),
            pltpu.VMEM((tiles, shards - 1, block_rows, tile), jnp.bfloat16),
            pltpu.SemaphoreType.DMA((groups,)),
            pltpu.SemaphoreType.DMA((groups,)),
            pltpu.SemaphoreType.DMA((tiles,)),
            pltpu.SemaphoreType.DMA((tiles, shards - 1)),
            pltpu.SemaphoreType.DMA((tiles, shards - 1)),
        ],
        compiler_params=pltpu.CompilerParams(
            collective_id=0, has_side_effects=True, vmem_limit_bytes=63 * 1024 * 1024
        ),
        name="attend",
    )(shelf_ids, dialog_ids, slot_fill, queries, fresh, pages, o_weight)


def solution(mesh):
    in_specs = (
        P("replica", "tensor"),
        P("replica", None, "tensor"),
        P("replica", None, None, "tensor"),
        P("replica", None),
        P("replica"),
        P("tensor", None),
    )
    out_specs = P(("replica", "tensor"), None)
    return jax.shard_map(local, mesh=mesh, in_specs=in_specs, out_specs=out_specs, check_vma=False)
```

profile of v0, /device:TPU:27, one launch (start us, length us, event | category | flops | bytes accessed | tf_op | source)
XLA Modules:
  0.0 111.8 jit_solution(5323348528405712627)
XLA Ops:
  0.0 0.7 subtract_clamp_fusion
  0.7 0.1 min.12
  0.8 0.7 and_select_fusion
  1.5 0.1 eq.41
  1.6 0.1 fusion.1
  1.7 0.1 mul.40
  1.8 0.1 mul.37
  1.9 0.1 copy.17
  2.0 0.3 select_reduce_fusion
  2.2 0.7 copy.18
  2.9 5.4 %all-to-all-start = ((s32[8,1,3]{2,1,0:T(1,128)}), s32[8,1,3]{2,1,0:T(1,128)S(1)}, u32[]{:S(2)}, u32[]{:S(2)}) async-start(s32[8,1,3]{2,1,0:T(1,128)} %copy.18), calls=%async_computation | async-start | bytes 8192 | tf_op jit(solution)/shard_map/all_to_all | solution.py:237
  8.4 0.7 copy.24.fill_ref
  9.0 1.0 fusion.4
  10.1 0.6 pad_maximum_fusion.fresh_ref
  10.7 0.7 copy.23.dialog_ref
  11.4 5.7 %reshape.79.pool_ref = bf16[24,256,256]{2,1,0:T(8,128)(2,1)} reshape(bf16[24,128,2,256]{3,2,1,0:T(2,128)(2,1)} %param.8) | data formatting | bytes 6291456 | tf_op jit(solution)/shard_map/reshape | solution.py:238
  17.1 0.0 all-to-all-done
  17.1 0.0 copy-start
  17.1 0.6 copy-done
  17.7 92.4 %attend.1 = bf16[16,8192]{1,0:T(8,128)(2,1)} custom-call(s32[8,3]{1,0:T(8,128)} %bitcast.8, s32[8,3]{1,0:T(8,128)} %copy.23.dialog_ref, s32[8,3]{1,0:T(8,128)} %copy.24.fill_ref, bf16[64,2048]{1,0:T(8,128)(2,1)} %q_ref.1, bf16[2,64,256]{2,1,0:T(8,128)(2,1)} %pad_maximum_fusion.fresh_ref, bf16[24,256,256]{2,1,0:T(8,128)(2,1)} %reshape.79.pool_ref, ...), custom_call_target="tpu_custom_call" | custom-call | tf_op jit(solution)/shard_map/attend/pallas_call | solution.py:243
  110.1 1.7 %copy.31 = bf16[16,8192]{1,0:T(8,128)(2,1)} copy(bf16[16,8192]{1,0:T(8,128)(2,1)} %attend.1) | data formatting | bytes 524288
  (7 shorter events, 0.1 us)
Async XLA Ops:
  2.9 14.2 %all-to-all-start = ((s32[8,1,3]{2,1,0:T(1,128)}), s32[8,1,3]{2,1,0:T(1,128)S(1)}, u32[]{:S(2)}, u32[]{:S(2)}) async-start(s32[8,1,3]{2,1,0:T(1,128)} %copy.18), calls=%async_computation | async-start | bytes 8192 | tf_op jit(solution)/shard_map/all_to_all | solution.py:237
  17.1 0.6 copy-start
where the time goes:
time: 112 us
  Pallas kernels  92.4 us (82%)
  local copies, waits for them, and re-layouts  11.5 us (10%)
  starting transfers between devices  5.44 us (5%)
  other arithmetic  2.46 us (2%)
    pallas_call x1, Pallas kernels, local(): pl.pallas_call(functools.partial(kernel, groups, shards, new_len), out_sh...  92.4 us
    reshape x1, local copies, waits for them, and re-layouts, local(): pages = pool.reshape(pool_size, 2 * page_len, kv_width)  5.74 us
    all_to_all x1, starting transfers between devices, local(): lax.all_to_all(wanted, 'replica', split_axis=0, concat_axis=0, tiled=True)  5.44 us
    unnamed x3, local copies, waits for them, and re-layouts  2.26 us
  transfers between devices with their start and end apart: 1, of which 0 were waited for; matrix products, arithmetic and copies ran while one was open for 8% of the time, Pallas kernels for 0%

commit v1 on v0

v1 whole, which is shorter than its diff:
```python
import functools
import math

import jax
import jax.numpy as jnp
from jax import lax
from jax.experimental import pallas as pl
from jax.experimental.pallas import tpu as pltpu
from jax.sharding import PartitionSpec as P

HD = 128
PAGE = 128
SLOT = 3
TILE = 1024
CORES = 2

floor_value = -1e30
tiny_value = 1e-30

MESH = pl.DeviceIdType.MESH
CONTRACT = (((1,), (1,)), ((), ()))


def spread(groups):
    outer = 1
    while outer * outer < groups:
        outer *= 2
    return outer, groups // outer


def selection(rows, kv_count):
    kinds = 2 * kv_count
    tokens = rows // kinds
    i = lax.broadcasted_iota(jnp.int32, (rows, rows), 0)
    j = lax.broadcasted_iota(jnp.int32, (rows, rows), 1)
    source = (i % tokens) * kinds + i // tokens
    return jnp.where(source == j, 1.0, 0.0).astype(jnp.bfloat16)


def kernel(
    groups, shards,
    q_hbm, fresh_hbm, pool_hbm, table_hbm, length_hbm, weight,
    out_ref,
    table, length, listed, pool_ref, fresh_ref, outgoing, arrived, wbuf, perm, qall, qcur, kbuf, vbuf,
    peak_ref, amount_ref, summed_ref, back, back_log, came, came_log, attended, part, sibling, joined, landed,
    load_sem, q_load_sem, weight_sem,
    table_send, table_recv, length_send, length_recv,
    q_send, q_recv, page_send, page_recv,
    back_send, back_recv, log_send, log_recv,
    core_send, core_recv, part_send, part_recv,
):
    outer, inner = spread(groups)
    half = outer // 2
    me = lax.axis_index("replica")
    mine = lax.axis_index("tensor")
    z = me // inner
    x = me % inner
    pool_size = pool_ref.shape[0]
    _, kv_count, dialogs, rows, _ = qall.shape
    entries = table.shape[2]
    token_rows = q_hbm.shape[0]
    new_len = token_rows // dialogs
    per_group = rows // new_len
    tiles, _, chips, block_rows, tile = part.shape
    block = perm.shape[0]
    page_rows = pool_ref.shape[1]
    block_tokens = block // (2 * kv_count)
    scale = math.log2(math.e) / math.sqrt(HD)
    chip = mine // CORES
    core = mine % CORES

    loads = [
        pltpu.make_async_copy(table_hbm, table.at[me], load_sem.at[0]),
        pltpu.make_async_copy(length_hbm, length.at[me], load_sem.at[1]),
        pltpu.make_async_copy(pool_hbm, pool_ref, load_sem.at[2]),
        pltpu.make_async_copy(fresh_hbm, fresh_ref, load_sem.at[3]),
    ]

    def q_load(k, d, g):
        col = (k * per_group + g) * HD
        return pltpu.make_async_copy(
            q_hbm.at[d * new_len : (d + 1) * new_len, col : col + HD],
            qall.at[z, k, d, g * new_len : (g + 1) * new_len, :],
            q_load_sem.at[k, d, g],
        )

    q_loads = [
        q_load(k, d, g) for k in range(kv_count) for d in range(dialogs) for g in range(per_group)
    ]

    loads[0].start()
    loads[1].start()
    for copy in q_loads:
        copy.start()
    loads[2].start()
    loads[3].start()

    barrier = pltpu.get_barrier_semaphore()
    for step in range(1, groups):
        pl.semaphore_signal(
            barrier, inc=1, device_id={"replica": lax.rem(me + step, groups)}, device_id_type=MESH
        )
    for step in range(1, shards):
        pl.semaphore_signal(
            barrier, inc=1, device_id={"tensor": lax.rem(mine + step, shards)}, device_id_type=MESH
        )

    def table_copy(step):
        return pltpu.make_async_remote_copy(
            src_ref=table.at[me],
            dst_ref=table.at[me],
            send_sem=table_send.at[step],
            recv_sem=table_recv.at[step],
            device_id={"replica": lax.rem(me + step, groups)},
            device_id_type=MESH,
        )

    def length_copy(step):
        return pltpu.make_async_remote_copy(
            src_ref=length.at[me],
            dst_ref=length.at[me],
            send_sem=length_send.at[step],
            recv_sem=length_recv.at[step],
            device_id={"replica": lax.rem(me + step, groups)},
            device_id_type=MESH,
        )

    def q_copy(group, k, way):
        dest = z + (1 if way == 0 else -1)
        return pltpu.make_async_remote_copy(
            src_ref=qall.at[group, k],
            dst_ref=qall.at[group, k],
            send_sem=q_send.at[way, group, k],
            recv_sem=q_recv.at[group, k],
            device_id={"replica": dest * inner + x},
            device_id_type=MESH,
        )

    def page_copy(step, group):
        return pltpu.make_async_remote_copy(
            src_ref=outgoing.at[step - 1, group],
            dst_ref=arrived.at[step - 1, group],
            send_sem=page_send.at[step - 1, group],
            recv_sem=page_recv.at[step - 1, group],
            device_id={"replica": z * inner + lax.rem(x + step, inner)},
            device_id_type=MESH,
        )

    def back_copy(group):
        return pltpu.make_async_remote_copy(
            src_ref=back.at[group],
            dst_ref=came.at[z],
            send_sem=back_send.at[group],
            recv_sem=back_recv.at[z],
            device_id={"replica": group * inner + x},
            device_id_type=MESH,
        )

    def log_copy(group):
        return pltpu.make_async_remote_copy(
            src_ref=back_log.at[group],
            dst_ref=came_log.at[z],
            send_sem=log_send.at[group],
            recv_sem=log_recv.at[z],
            device_id={"replica": group * inner + x},
            device_id_type=MESH,
        )

    def weight_copy(index):
        return pltpu.make_async_copy(
            weight.at[:, pl.ds(pl.multiple_of(index * tile, tile), tile)],
            wbuf.at[index],
            weight_sem.at[index],
        )

    def core_copy(index):
        return pltpu.make_async_remote_copy(
            src_ref=part.at[index, 1 - core],
            dst_ref=sibling.at[index],
            send_sem=core_send.at[index],
            recv_sem=core_recv.at[index],
            device_id={"tensor": chip * CORES + 1 - core},
            device_id_type=MESH,
        )

    def part_copy(index, step):
        dest = lax.rem(chip + step, chips)
        return pltpu.make_async_remote_copy(
            src_ref=joined.at[index, step - 1],
            dst_ref=landed.at[index, step - 1],
            send_sem=part_send.at[index, step - 1],
            recv_sem=part_recv.at[index, step - 1],
            device_id={"tensor": dest * CORES + core},
            device_id_type=MESH,
        )

    perm[...] = selection(block, kv_count)

    side = z // half

    def served(turn):
        across = (1 - side) * (half + turn) + side * (half - 1 - turn)
        beside = side * half + lax.rem(z - side * half + 1 + turn - half + outer, half)
        far = (turn < half).astype(jnp.int32) if not isinstance(turn, int) else int(turn < half)
        return far * across + (1 - far) * beside

    loads[0].wait()
    loads[1].wait()
    pl.semaphore_wait(barrier, groups + shards - 2)
    for step in range(1, groups):
        table_copy(step).start()
        length_copy(step).start()
    for copy in q_loads:
        copy.wait()
    for k in range(kv_count):
        @pl.when(z < outer - 1)
        def _():
            q_copy(z, k, 0).start()

        @pl.when(z > 0)
        def _():
            q_copy(z, k, 1).start()

    loads[2].wait()
    loads[3].wait()
    for step in range(1, groups):
        table_copy(step).wait_recv()
        length_copy(step).wait_recv()

    def request(group, owner):
        count = jnp.int32(0)
        zero = jnp.int32(0)
        shelf, dialog, fill = [zero] * SLOT, [zero] * SLOT, [zero] * SLOT
        low = owner * pool_size
        for d in range(dialogs):
            total = length[group, d]
            for e in range(entries):
                place = table[group, d, e] - low
                live = jnp.minimum(total - e * PAGE, PAGE)
                hit = (place >= 0) & (place < pool_size) & (live > 0)
                for s in range(SLOT):
                    here = hit & (count == s)
                    shelf[s] = jnp.where(here, place, shelf[s])
                    dialog[s] = jnp.where(here, d, dialog[s])
                    fill[s] = jnp.where(here, live, fill[s])
                count = count + hit.astype(jnp.int32)
        return shelf, dialog, fill

    def send_pages(turn, carry):
        group = served(turn)
        for step in range(1, inner):
            shelf, _, _ = request(group * inner + lax.rem(x + step, inner), me)
            for s in range(SLOT):
                outgoing[step - 1, group, s] = pool_ref[shelf[s]]
            page_copy(step, group).start()
        return carry

    lax.fori_loop(0, outer, send_pages, 0)

    for index in range(tiles):
        weight_copy(index).start()

    def list_pages(group, carry):
        for step in range(inner):
            shelf, dialog, fill = request(
                group * inner + x, z * inner + lax.rem(x - step + inner, inner)
            )
            for s in range(SLOT):
                listed[group, step, s, 0] = shelf[s]
                listed[group, step, s, 1] = dialog[s]
                listed[group, step, s, 2] = fill[s]
        return carry

    lax.fori_loop(0, outer, list_pages, 0)

    fresh_rows = fresh_ref.shape[0]
    split = jnp.dot(
        selection(fresh_rows, kv_count), fresh_ref[...], preferred_element_type=jnp.float32
    ).astype(jnp.bfloat16)
    row_token = lax.broadcasted_iota(jnp.int32, (rows, token_rows), 0) % new_len
    col_token = lax.broadcasted_iota(jnp.int32, (rows, token_rows), 1)
    for k in range(kv_count):
        keys = split[(2 * k) * token_rows : (2 * k + 1) * token_rows]
        values = split[(2 * k + 1) * token_rows : (2 * k + 2) * token_rows]
        for d in range(dialogs):
            scores = lax.dot_general(
                qall[z, k, d], keys, CONTRACT, preferred_element_type=jnp.float32
            ) * scale
            causal = (col_token // new_len == d) & (col_token - d * new_len <= row_token)
            scores = jnp.where(causal, scores, floor_value)
            peak = jnp.max(scores, axis=-1, keepdims=True)
            weights = jnp.exp2(scores - peak).astype(jnp.bfloat16)
            peak_ref[z, k, d] = jnp.broadcast_to(peak, (rows, HD))
            amount_ref[z, k, d] = jnp.broadcast_to(
                jnp.sum(weights.astype(jnp.float32), axis=-1, keepdims=True), (rows, HD)
            )
            summed_ref[z, k, d] = jnp.dot(weights, values, preferred_element_type=jnp.float32)

    def absorb(group, step, fetch, first):
        position = lax.broadcasted_iota(jnp.int32, (rows, PAGE), 1)
        dialog, fill = [], []
        for s in range(SLOT):
            dialog.append(listed[group, step, s, 1])
            fill.append(listed[group, step, s, 2])
            for b in range(page_rows // block):
                split = jnp.dot(
                    perm[...], fetch(s, b), preferred_element_type=jnp.float32
                ).astype(jnp.bfloat16)
                at = s * PAGE + b * block_tokens
                for k in range(kv_count):
                    low = 2 * k * block_tokens
                    kbuf[k, at : at + block_tokens, :] = split[low : low + block_tokens]
                    vbuf[k, at : at + block_tokens, :] = split[
                        low + block_tokens : low + 2 * block_tokens
                    ]
        owned = [
            [jnp.broadcast_to(dialog[s], (rows, HD)) == d for d in range(dialogs)]
            for s in range(SLOT)
        ]
        for k in range(kv_count):
            for d in range(dialogs):
                qcur[k, d] = qall[group, k, d]
            scores, highs = [], []
            for s in range(SLOT):
                keys = kbuf[k, s * PAGE : (s + 1) * PAGE, :]
                found = lax.dot_general(
                    qcur[k, dialog[s]], keys, CONTRACT, preferred_element_type=jnp.float32
                ) * scale
                found = jnp.where(position < fill[s], found, floor_value)
                scores.append(found)
                highs.append(
                    jnp.broadcast_to(jnp.max(found, axis=-1, keepdims=True), (rows, HD))
                )
            peaks, keeps = [], []
            for d in range(dialogs):
                peak = functools.reduce(
                    jnp.maximum,
                    [jnp.where(owned[s][d], highs[s], floor_value) for s in range(SLOT)],
                )
                if not first:
                    before = peak_ref[group, k, d]
                    peak = jnp.maximum(peak, before)
                    keeps.append(jnp.exp2(before - peak))
                peaks.append(peak)
                peak_ref[group, k, d] = peak
            amounts, sums = [], []
            for s in range(SLOT):
                peak = peaks[-1]
                for d in reversed(range(dialogs - 1)):
                    peak = jnp.where(owned[s][d], peaks[d], peak)
                weights = jnp.exp2(scores[s] - peak).astype(jnp.bfloat16)
                values = vbuf[k, s * PAGE : (s + 1) * PAGE, :]
                amounts.append(
                    jnp.broadcast_to(
                        jnp.sum(weights.astype(jnp.float32), axis=-1, keepdims=True), (rows, HD)
                    )
                )
                sums.append(jnp.dot(weights, values, preferred_element_type=jnp.float32))
            for d in range(dialogs):
                amount = functools.reduce(
                    jnp.add, [jnp.where(owned[s][d], amounts[s], 0.0) for s in range(SLOT)]
                )
                total = functools.reduce(
                    jnp.add, [jnp.where(owned[s][d], sums[s], 0.0) for s in range(SLOT)]
                )
                if not first:
                    amount = amount + keeps[d] * amount_ref[group, k, d]
                    total = total + keeps[d] * summed_ref[group, k, d]
                amount_ref[group, k, d] = amount
                summed_ref[group, k, d] = total

    def absorb_own(group, first):
        shelf = [listed[group, 0, s, 0] for s in range(SLOT)]
        absorb(
            group, 0, lambda s, b: pool_ref[shelf[s], b * block : (b + 1) * block, :], first
        )

    def absorb_arrived(group):
        for step in range(1, inner):
            page_copy(step, group).wait_recv()
            absorb(
                group,
                step,
                lambda s, b: arrived[step - 1, group, s, b * block : (b + 1) * block, :],
                False,
            )

    absorb_own(z, False)

    def relay(distance):
        for k in range(kv_count):
            @pl.when(z >= distance)
            def _():
                q_copy(z - distance, k, 0).wait_recv()

            @pl.when((z >= distance) & (z < outer - 1))
            def _():
                q_copy(z - distance, k, 0).start()

            @pl.when(z < outer - distance)
            def _():
                q_copy(z + distance, k, 1).wait_recv()

            @pl.when((z < outer - distance) & (z > 0))
            def _():
                q_copy(z + distance, k, 1).start()

    def serve(turn, carry):
        group = served(turn)
        absorb_own(group, True)
        absorb_arrived(group)
        for k in range(kv_count):
            for d in range(dialogs):
                amount = jnp.maximum(amount_ref[group, k, d], tiny_value)
                back[group, k, d] = (summed_ref[group, k, d] / amount).astype(jnp.bfloat16)
                log = peak_ref[group, k, d] + jnp.log2(amount)
                back_log[group, pl.ds(k * dialogs + d, 1), :] = jnp.transpose(log)[:1]
        back_copy(group).start()
        log_copy(group).start()
        return carry

    for distance in range(1, half + 1):
        relay(distance)
    lax.fori_loop(0, 1, serve, 0)
    for distance in range(half + 1, outer):
        relay(distance)
    lax.fori_loop(1, outer - 1, serve, 0)

    def merge(turn, carry):
        source = served(turn)
        back_copy_in(source)
        for k in range(kv_count):
            for d in range(dialogs):
                line = came_log[source, pl.ds(k * dialogs + d, 1), :]
                log = jnp.transpose(jnp.broadcast_to(line, (HD, rows)))
                before = peak_ref[z, k, d]
                peak = jnp.maximum(before, log)
                keep = jnp.exp2(before - peak)
                take = jnp.exp2(log - peak)
                peak_ref[z, k, d] = peak
                amount_ref[z, k, d] = keep * amount_ref[z, k, d] + take
                summed_ref[z, k, d] = keep * summed_ref[z, k, d] + take * came[
                    source, k, d
                ].astype(jnp.float32)
        return carry

    def back_copy_in(source):
        pltpu.make_async_remote_copy(
            src_ref=back.at[source],
            dst_ref=came.at[source],
            send_sem=back_send.at[source],
            recv_sem=back_recv.at[source],
            device_id={"replica": source * inner + x},
            device_id_type=MESH,
        ).wait_recv()
        pltpu.make_async_remote_copy(
            src_ref=back_log.at[source],
            dst_ref=came_log.at[source],
            send_sem=log_send.at[source],
            recv_sem=log_recv.at[source],
            device_id={"replica": source * inner + x},
            device_id_type=MESH,
        ).wait_recv()

    lax.fori_loop(0, half, merge, 0)
    absorb_arrived(z)
    lax.fori_loop(half, outer - 1, merge, 0)

    for k in range(kv_count):
        for d in range(dialogs):
            ratio = (summed_ref[z, k, d] / amount_ref[z, k, d]).astype(jnp.bfloat16)
            for g in range(per_group):
                col = (k * per_group + g) * HD
                attended[d * new_len : (d + 1) * new_len, col : col + HD] = ratio[
                    g * new_len : (g + 1) * new_len
                ]

    def join(index):
        core_copy(index).wait_recv()
        for step in range(1, chips):
            dest = lax.rem(chip + step, chips)
            total = part[index, core, dest].astype(jnp.float32) + sibling[index, dest].astype(
                jnp.float32
            )
            joined[index, step - 1] = total.astype(jnp.bfloat16)
            part_copy(index, step).start()

    def project(index, carry):
        weight_copy(index).wait()
        product = jnp.dot(attended[...], wbuf[index], preferred_element_type=jnp.float32)
        product = product.astype(jnp.bfloat16)
        for dest in range(shards):
            part[index, dest % CORES, dest // CORES] = product[
                dest * block_rows : (dest + 1) * block_rows
            ]
        core_copy(index).start()

        @pl.when(index > 0)
        def _():
            join(index - 1)

        return carry

    lax.fori_loop(0, tiles, project, 0)
    join(tiles - 1)

    def finish(index, carry):
        total = part[index, core, chip].astype(jnp.float32) + sibling[index, chip].astype(
            jnp.float32
        )
        for step in range(1, chips):
            part_copy(index, step).wait_recv()
            total = total + landed[index, step - 1].astype(jnp.float32)
        out_ref[:, pl.ds(pl.multiple_of(index * tile, tile), tile)] = total.astype(out_ref.dtype)
        return carry

    lax.fori_loop(0, tiles, finish, 0)

    def drain(index, carry):
        core_copy(index).wait_send()
        for step in range(1, chips):
            part_copy(index, step).wait_send()
        return carry

    lax.fori_loop(0, tiles, drain, 0)

    def drain_back(turn, carry):
        back_copy(served(turn)).wait_send()
        log_copy(served(turn)).wait_send()
        return carry

    lax.fori_loop(0, outer - 1, drain_back, 0)

    def drain_line(group, carry):
        for step in range(1, inner):
            page_copy(step, group).wait_send()
        for k in range(kv_count):
            @pl.when((group <= z) & (z < outer - 1))
            def _():
                q_copy(group, k, 0).wait_send()

            @pl.when((group >= z) & (z > 0))
            def _():
                q_copy(group, k, 1).wait_send()

        return carry

    lax.fori_loop(0, outer, drain_line, 0)
    for step in range(1, groups):
        table_copy(step).wait_send()
        length_copy(step).wait_send()


def local(queries, kv_new, pool, page_table, hist_len, o_weight):
    groups = lax.axis_size("replica")
    shards = lax.axis_size("tensor")
    outer, inner = spread(groups)
    pool_size, page_len, _, kv_width = pool.shape
    dialogs, entries = page_table.shape
    token_rows = queries.shape[0]
    new_len = token_rows // dialogs
    kv_count = kv_width // HD
    per_group = queries.shape[1] // kv_width
    rows = per_group * new_len
    depth, model = o_weight.shape
    tile = min(TILE, model)
    tiles = model // tile
    block_rows = token_rows // shards
    chips = shards // CORES
    page_rows = 2 * kv_count * page_len
    block = 256
    pages = pool.reshape(pool_size, page_len, 2, kv_count, HD).transpose(0, 1, 3, 2, 4)
    pages = pages.reshape(pool_size, page_rows, HD)
    fresh = kv_new.reshape(token_rows, 2, kv_count, HD).transpose(0, 2, 1, 3)
    fresh = fresh.reshape(2 * kv_count * token_rows, HD)
    vmem = pl.BlockSpec(memory_space=pltpu.VMEM)
    anywhere = pl.BlockSpec(memory_space=pl.ANY)
    dma = pltpu.SemaphoreType.DMA
    bf16, f32 = jnp.bfloat16, jnp.float32
    return pl.pallas_call(
        functools.partial(kernel, groups, shards),
        out_shape=jax.ShapeDtypeStruct((block_rows, model), jnp.bfloat16),
        in_specs=[anywhere] * 6,
        out_specs=vmem,
        scratch_shapes=[
            pltpu.SMEM((groups, dialogs, entries), jnp.int32),
            pltpu.SMEM((groups, dialogs), jnp.int32),
            pltpu.SMEM((outer, inner, SLOT, 3), jnp.int32),
            pltpu.VMEM((pool_size, page_rows, HD), bf16),
            pltpu.VMEM((2 * kv_count * token_rows, HD), bf16),
            pltpu.VMEM((inner - 1, outer, SLOT, page_rows, HD), bf16),
            pltpu.VMEM((inner - 1, outer, SLOT, page_rows, HD), bf16),
            pltpu.VMEM((tiles, depth, tile), bf16),
            pltpu.VMEM((block, block), bf16),
            pltpu.VMEM((outer, kv_count, dialogs, rows, HD), bf16),
            pltpu.VMEM((kv_count, dialogs, rows, HD), bf16),
            pltpu.VMEM((kv_count, SLOT * page_len, HD), bf16),
            pltpu.VMEM((kv_count, SLOT * page_len, HD), bf16),
            pltpu.VMEM((outer, kv_count, dialogs, rows, HD), f32),
            pltpu.VMEM((outer, kv_count, dialogs, rows, HD), f32),
            pltpu.VMEM((outer, kv_count, dialogs, rows, HD), f32),
            pltpu.VMEM((outer, kv_count, dialogs, rows, HD), bf16),
            pltpu.VMEM((outer, kv_count * dialogs, rows), f32),
            pltpu.VMEM((outer, kv_count, dialogs, rows, HD), bf16),
            pltpu.VMEM((outer, kv_count * dialogs, rows), f32),
            pltpu.VMEM((token_rows, depth), bf16),
            pltpu.VMEM((tiles, CORES, chips, block_rows, tile), bf16),
            pltpu.VMEM((tiles, chips, block_rows, tile), bf16),
            pltpu.VMEM((tiles, chips - 1, block_rows, tile), bf16),
            pltpu.VMEM((tiles, chips - 1, block_rows, tile), bf16),
            dma((4,)),
            dma((kv_count, dialogs, per_group)),
            dma((tiles,)),
            dma((groups,)),
            dma((groups,)),
            dma((groups,)),
            dma((groups,)),
            dma((2, outer, kv_count)),
            dma((outer, kv_count)),
            dma((inner - 1, outer)),
            dma((inner - 1, outer)),
            dma((outer,)),
            dma((outer,)),
            dma((outer,)),
            dma((outer,)),
            dma((tiles,)),
            dma((tiles,)),
            dma((tiles, chips - 1)),
            dma((tiles, chips - 1)),
        ],
        compiler_params=pltpu.CompilerParams(
            collective_id=0, has_side_effects=True, vmem_limit_bytes=63 * 1024 * 1024
        ),
        name="attend",
    )(queries, fresh, pages, page_table, hist_len, o_weight)


def solution(mesh):
    in_specs = (
        P("replica", "tensor"),
        P("replica", None, "tensor"),
        P("replica", None, None, "tensor"),
        P("replica", None),
        P("replica"),
        P("tensor", None),
    )
    out_specs = P(("replica", "tensor"), None)
    return jax.shard_map(local, mesh=mesh, in_specs=in_specs, out_specs=out_specs, check_vma=False)
```

time: 112 us -> 65.7 us (0.59)
  the two profiles are of different devices: /device:TPU:27 before, /device:TPU:0 now
where the time goes in v1:
time: 65.7 us; the launch traced here: 65.6 us
  Pallas kernels  63.9 us (97%)
  local copies, waits for them, and re-layouts  1.67 us (3%)
    pallas_call x1, Pallas kernels, local(): pl.pallas_call(functools.partial(kernel, groups, shards), out_shape=jax.S...  63.9 us
    unnamed x1, local copies, waits for them, and re-layouts  1.67 us

profile of v1, /device:TPU:0, one launch (start us, length us, event | category | flops | bytes accessed | tf_op | source)
XLA Modules:
  0.0 65.6 jit_solution(9653988866067717611)
XLA Ops:
  0.0 63.9 %attend.1 = bf16[16,8192]{1,0:T(8,128)(2,1)} custom-call(bf16[64,2048]{1,0:T(8,128)(2,1)} %q_hbm.1, bf16[256,128]{1,0:T(8,128)(2,1)} %bitcast.11, bf16[24,512,128]{2,1,0:T(8,128)(2,1)} %bitcast.10, s32[2,12]{1,0:T(2,128)} %table_hbm.1, s32[2]{0:T(128)} %length_hbm.1, bf16[2048,8192]{1,0:T(8,128)(2,1)} %weight.1), custom_call_target="tpu_custom_call" | custom-call | tf_op jit(solution)/shard_map/attend/pallas_call | solution.py:580
  63.9 1.7 %copy.10 = bf16[16,8192]{1,0:T(8,128)(2,1)} copy(bf16[16,8192]{1,0:T(8,128)(2,1)} %attend.1) | data formatting | bytes 524288

commit v2 on v1

--- a/solution.py
+++ b/solution.py
@@ -11,7 +11,8 @@
 HD = 128
 PAGE = 128
 SLOT = 3
-TILE = 1024
+TILE = 512
+LAG = 4
 CORES = 2
 
 floor_value = -1e30
@@ -41,8 +42,9 @@
     groups, shards,
     q_hbm, fresh_hbm, pool_hbm, table_hbm, length_hbm, weight,
     out_ref,
-    table, length, listed, pool_ref, fresh_ref, outgoing, arrived, wbuf, perm, qall, qcur, kbuf, vbuf,
-    peak_ref, amount_ref, summed_ref, back, back_log, came, came_log, attended, part, sibling, joined, landed,
+    table, length, listed, pool_ref, fresh_ref, kept, outgoing, arrived, wbuf, perm, qall, qcur,
+    peak_ref, amount_ref, summed_ref, back, back_log, came, came_log, attended, gathered,
+    part, sibling, joined, landed,
     load_sem, q_load_sem, weight_sem,
     table_send, table_recv, length_send, length_recv,
     q_send, q_recv, page_send, page_recv,
@@ -136,32 +138,32 @@
             device_id_type=MESH,
         )
 
-    def page_copy(step, group):
-        return pltpu.make_async_remote_copy(
-            src_ref=outgoing.at[step - 1, group],
-            dst_ref=arrived.at[step - 1, group],
-            send_sem=page_send.at[step - 1, group],
-            recv_sem=page_recv.at[step - 1, group],
+    def page_copy(step, group, k):
+        return pltpu.make_async_remote_copy(
+            src_ref=outgoing.at[step - 1, group, k],
+            dst_ref=arrived.at[step - 1, group, k],
+            send_sem=page_send.at[step - 1, group, k],
+            recv_sem=page_recv.at[step - 1, group, k],
             device_id={"replica": z * inner + lax.rem(x + step, inner)},
             device_id_type=MESH,
         )
 
-    def back_copy(group):
-        return pltpu.make_async_remote_copy(
-            src_ref=back.at[group],
-            dst_ref=came.at[z],
-            send_sem=back_send.at[group],
-            recv_sem=back_recv.at[z],
+    def back_copy(group, k, source):
+        return pltpu.make_async_remote_copy(
+            src_ref=back.at[group, k],
+            dst_ref=came.at[source, k],
+            send_sem=back_send.at[group, k],
+            recv_sem=back_recv.at[source, k],
             device_id={"replica": group * inner + x},
             device_id_type=MESH,
         )
 
-    def log_copy(group):
-        return pltpu.make_async_remote_copy(
-            src_ref=back_log.at[group],
-            dst_ref=came_log.at[z],
-            send_sem=log_send.at[group],
-            recv_sem=log_recv.at[z],
+    def log_copy(group, k, source):
+        return pltpu.make_async_remote_copy(
+            src_ref=back_log.at[group, k],
+            dst_ref=came_log.at[source, k],
+            send_sem=log_send.at[group, k],
+            recv_sem=log_recv.at[source, k],
             device_id={"replica": group * inner + x},
             device_id_type=MESH,
         )
@@ -223,9 +225,6 @@
 
     loads[2].wait()
     loads[3].wait()
-    for step in range(1, groups):
-        table_copy(step).wait_recv()
-        length_copy(step).wait_recv()
 
     def request(group, owner):
         count = jnp.int32(0)
@@ -246,13 +245,41 @@
                 count = count + hit.astype(jnp.int32)
         return shelf, dialog, fill
 
+    def await_tables(group):
+        for other in range(inner):
+            source = group * inner + other
+            step = lax.rem(me - source + groups, groups)
+
+            @pl.when(source != me)
+            def _():
+                table_copy(step).wait_recv()
+                length_copy(step).wait_recv()
+
+    def separate(shelf, put):
+        for s in range(SLOT):
+            for b in range(page_rows // block):
+                split = jnp.dot(
+                    perm[...],
+                    pool_ref[shelf[s], b * block : (b + 1) * block, :],
+                    preferred_element_type=jnp.float32,
+                ).astype(jnp.bfloat16)
+                for k in range(kv_count):
+                    for kind in range(2):
+                        low = (2 * k + kind) * block_tokens
+                        put(k, s, kind, b * block_tokens, split[low : low + block_tokens])
+
     def send_pages(turn, carry):
         group = served(turn)
+        await_tables(group)
         for step in range(1, inner):
             shelf, _, _ = request(group * inner + lax.rem(x + step, inner), me)
-            for s in range(SLOT):
-                outgoing[step - 1, group, s] = pool_ref[shelf[s]]
-            page_copy(step, group).start()
+
+            def put(k, s, kind, at, rows_of):
+                outgoing[step - 1, group, k, s, kind, at : at + block_tokens, :] = rows_of
+
+            separate(shelf, put)
+            for k in range(kv_count):
+                page_copy(step, group, k).start()
         return carry
 
     lax.fori_loop(0, outer, send_pages, 0)
@@ -266,9 +293,14 @@
                 group * inner + x, z * inner + lax.rem(x - step + inner, inner)
             )
             for s in range(SLOT):
-                listed[group, step, s, 0] = shelf[s]
-                listed[group, step, s, 1] = dialog[s]
-                listed[group, step, s, 2] = fill[s]
+                listed[group, step, s, 0] = dialog[s]
+                listed[group, step, s, 1] = fill[s]
+            if step == 0:
+
+                def put(k, s, kind, at, rows_of):
+                    kept[group, k, s, kind, at : at + block_tokens, :] = rows_of
+
+                separate(shelf, put)
         return carry
 
     lax.fori_loop(0, outer, list_pages, 0)
@@ -296,96 +328,74 @@
             )
             summed_ref[z, k, d] = jnp.dot(weights, values, preferred_element_type=jnp.float32)
 
-    def absorb(group, step, fetch, first):
+    def absorb(group, k, step, pages, first):
         position = lax.broadcasted_iota(jnp.int32, (rows, PAGE), 1)
-        dialog, fill = [], []
-        for s in range(SLOT):
-            dialog.append(listed[group, step, s, 1])
-            fill.append(listed[group, step, s, 2])
-            for b in range(page_rows // block):
-                split = jnp.dot(
-                    perm[...], fetch(s, b), preferred_element_type=jnp.float32
-                ).astype(jnp.bfloat16)
-                at = s * PAGE + b * block_tokens
-                for k in range(kv_count):
-                    low = 2 * k * block_tokens
-                    kbuf[k, at : at + block_tokens, :] = split[low : low + block_tokens]
-                    vbuf[k, at : at + block_tokens, :] = split[
-                        low + block_tokens : low + 2 * block_tokens
-                    ]
+        dialog = [listed[group, step, s, 0] for s in range(SLOT)]
+        fill = [listed[group, step, s, 1] for s in range(SLOT)]
         owned = [
             [jnp.broadcast_to(dialog[s], (rows, HD)) == d for d in range(dialogs)]
             for s in range(SLOT)
         ]
-        for k in range(kv_count):
-            for d in range(dialogs):
-                qcur[k, d] = qall[group, k, d]
-            scores, highs = [], []
-            for s in range(SLOT):
-                keys = kbuf[k, s * PAGE : (s + 1) * PAGE, :]
-                found = lax.dot_general(
-                    qcur[k, dialog[s]], keys, CONTRACT, preferred_element_type=jnp.float32
-                ) * scale
-                found = jnp.where(position < fill[s], found, floor_value)
-                scores.append(found)
-                highs.append(
-                    jnp.broadcast_to(jnp.max(found, axis=-1, keepdims=True), (rows, HD))
+        for d in range(dialogs):
+            qcur[d] = qall[group, k, d]
+        scores, highs = [], []
+        for s in range(SLOT):
+            found = lax.dot_general(
+                qcur[dialog[s]], pages[s, 0], CONTRACT, preferred_element_type=jnp.float32
+            ) * scale
+            found = jnp.where(position < fill[s], found, floor_value)
+            scores.append(found)
+            highs.append(jnp.broadcast_to(jnp.max(found, axis=-1, keepdims=True), (rows, HD)))
+        peaks, keeps = [], []
+        for d in range(dialogs):
+            peak = functools.reduce(
+                jnp.maximum,
+                [jnp.where(owned[s][d], highs[s], floor_value) for s in range(SLOT)],
+            )
+            if not first:
+                before = peak_ref[group, k, d]
+                peak = jnp.maximum(peak, before)
+                keeps.append(jnp.exp2(before - peak))
+            peaks.append(peak)
+            peak_ref[group, k, d] = peak
+        amounts, sums = [], []
+        for s in range(SLOT):
+            peak = peaks[-1]
+            for d in reversed(range(dialogs - 1)):
+                peak = jnp.where(owned[s][d], peaks[d], peak)
+            weights = jnp.exp2(scores[s] - peak).astype(jnp.bfloat16)
+            amounts.append(
+                jnp.broadcast_to(
+                    jnp.sum(weights.astype(jnp.float32), axis=-1, keepdims=True), (rows, HD)
                 )
-            peaks, keeps = [], []
-            for d in range(dialogs):
-                peak = functools.reduce(
-                    jnp.maximum,
-                    [jnp.where(owned[s][d], highs[s], floor_value) for s in range(SLOT)],
-                )
-                if not first:
-                    before = peak_ref[group, k, d]
-                    peak = jnp.maximum(peak, before)
-                    keeps.append(jnp.exp2(before - peak))
-                peaks.append(peak)
-                peak_ref[group, k, d] = peak
-            amounts, sums = [], []
-            for s in range(SLOT):
-                peak = peaks[-1]
-                for d in reversed(range(dialogs - 1)):
-                    peak = jnp.where(owned[s][d], peaks[d], peak)
-                weights = jnp.exp2(scores[s] - peak).astype(jnp.bfloat16)
-                values = vbuf[k, s * PAGE : (s + 1) * PAGE, :]
-                amounts.append(
-                    jnp.broadcast_to(
-                        jnp.sum(weights.astype(jnp.float32), axis=-1, keepdims=True), (rows, HD)
-                    )
-                )
-                sums.append(jnp.dot(weights, values, preferred_element_type=jnp.float32))
-            for d in range(dialogs):
-                amount = functools.reduce(
-                    jnp.add, [jnp.where(owned[s][d], amounts[s], 0.0) for s in range(SLOT)]
-                )
-                total = functools.reduce(
-                    jnp.add, [jnp.where(owned[s][d], sums[s], 0.0) for s in range(SLOT)]
-                )
-                if not first:
-                    amount = amount + keeps[d] * amount_ref[group, k, d]
-                    total = total + keeps[d] * summed_ref[group, k, d]
-                amount_ref[group, k, d] = amount
-                summed_ref[group, k, d] = total
-
-    def absorb_own(group, first):
-        shelf = [listed[group, 0, s, 0] for s in range(SLOT)]
-        absorb(
-            group, 0, lambda s, b: pool_ref[shelf[s], b * block : (b + 1) * block, :], first
-        )
-
-    def absorb_arrived(group):
+            )
+            sums.append(jnp.dot(weights, pages[s, 1], preferred_element_type=jnp.float32))
+        for d in range(dialogs):
+            amount = functools.reduce(
+                jnp.add, [jnp.where(owned[s][d], amounts[s], 0.0) for s in range(SLOT)]
+            )
+            total = functools.reduce(
+                jnp.add, [jnp.where(owned[s][d], sums[s], 0.0) for s in range(SLOT)]
+            )
+            if not first:
+                amount = amount + keeps[d] * amount_ref[group, k, d]
+                total = total + keeps[d] * summed_ref[group, k, d]
+            amount_ref[group, k, d] = amount
+            summed_ref[group, k, d] = total
+
+    def absorb_kept(group, k, first):
+        absorb(group, k, 0, kept.at[group, k], first)
+
+    def absorb_arrived(group, k):
         for step in range(1, inner):
-            page_copy(step, group).wait_recv()
-            absorb(
-                group,
-                step,
-                lambda s, b: arrived[step - 1, group, s, b * block : (b + 1) * block, :],
-                False,
-            )
-
-    absorb_own(z, False)
+            page_copy(step, group, k).wait_recv()
+            absorb(group, k, step, arrived.at[step - 1, group, k], False)
+
+    def begin(k, carry):
+        absorb_kept(z, k, False)
+        return carry
+
+    lax.fori_loop(0, kv_count, begin, 0)
 
     def relay(distance):
         for k in range(kv_count):
@@ -405,75 +415,80 @@
             def _():
                 q_copy(z + distance, k, 1).start()
 
-    def serve(turn, carry):
-        group = served(turn)
-        absorb_own(group, True)
-        absorb_arrived(group)
-        for k in range(kv_count):
-            for d in range(dialogs):
-                amount = jnp.maximum(amount_ref[group, k, d], tiny_value)
-                back[group, k, d] = (summed_ref[group, k, d] / amount).astype(jnp.bfloat16)
-                log = peak_ref[group, k, d] + jnp.log2(amount)
-                back_log[group, pl.ds(k * dialogs + d, 1), :] = jnp.transpose(log)[:1]
-        back_copy(group).start()
-        log_copy(group).start()
+    def serve(index, carry):
+        group = served(index // kv_count)
+        k = index % kv_count
+        absorb_kept(group, k, True)
+        absorb_arrived(group, k)
+        for d in range(dialogs):
+            amount = jnp.maximum(amount_ref[group, k, d], tiny_value)
+            back[group, k, d] = (summed_ref[group, k, d] / amount).astype(jnp.bfloat16)
+            log = peak_ref[group, k, d] + jnp.log2(amount)
+            back_log[group, k, d : d + 1, :] = jnp.transpose(log)[:1]
+        back_copy(group, k, z).start()
+        log_copy(group, k, z).start()
         return carry
 
     for distance in range(1, half + 1):
         relay(distance)
-    lax.fori_loop(0, 1, serve, 0)
+    lax.fori_loop(0, kv_count, serve, 0)
     for distance in range(half + 1, outer):
         relay(distance)
-    lax.fori_loop(1, outer - 1, serve, 0)
-
-    def merge(turn, carry):
+    lax.fori_loop(kv_count, (outer - 1) * kv_count, serve, 0)
+
+    def merge(turn, k):
         source = served(turn)
-        back_copy_in(source)
-        for k in range(kv_count):
-            for d in range(dialogs):
-                line = came_log[source, pl.ds(k * dialogs + d, 1), :]
-                log = jnp.transpose(jnp.broadcast_to(line, (HD, rows)))
-                before = peak_ref[z, k, d]
-                peak = jnp.maximum(before, log)
-                keep = jnp.exp2(before - peak)
-                take = jnp.exp2(log - peak)
-                peak_ref[z, k, d] = peak
-                amount_ref[z, k, d] = keep * amount_ref[z, k, d] + take
-                summed_ref[z, k, d] = keep * summed_ref[z, k, d] + take * came[
-                    source, k, d
-                ].astype(jnp.float32)
-        return carry
-
-    def back_copy_in(source):
-        pltpu.make_async_remote_copy(
-            src_ref=back.at[source],
-            dst_ref=came.at[source],
-            send_sem=back_send.at[source],
-            recv_sem=back_recv.at[source],
-            device_id={"replica": source * inner + x},
-            device_id_type=MESH,
-        ).wait_recv()
-        pltpu.make_async_remote_copy(
-            src_ref=back_log.at[source],
-            dst_ref=came_log.at[source],
-            send_sem=log_send.at[source],
-            recv_sem=log_recv.at[source],
-            device_id={"replica": source * inner + x},
-            device_id_type=MESH,
-        ).wait_recv()
-
-    lax.fori_loop(0, half, merge, 0)
-    absorb_arrived(z)
-    lax.fori_loop(half, outer - 1, merge, 0)
-
-    for k in range(kv_count):
+        back_copy(source, k, source).wait_recv()
+        log_copy(source, k, source).wait_recv()
+        for d in range(dialogs):
+            line = came_log[source, k, d : d + 1, :]
+            log = jnp.transpose(jnp.broadcast_to(line, (HD, rows)))
+            before = peak_ref[z, k, d]
+            peak = jnp.maximum(before, log)
+            keep = jnp.exp2(before - peak)
+            take = jnp.exp2(log - peak)
+            peak_ref[z, k, d] = peak
+            amount_ref[z, k, d] = keep * amount_ref[z, k, d] + take
+            summed_ref[z, k, d] = keep * summed_ref[z, k, d] + take * came[
+                source, k, d
+            ].astype(jnp.float32)
+        return k
+
+    head_depth = per_group * HD
+
+    def complete(k, carry):
+        lax.fori_loop(0, half, merge, k)
+        absorb_arrived(z, k)
+        lax.fori_loop(half, outer - 1, merge, k)
         for d in range(dialogs):
             ratio = (summed_ref[z, k, d] / amount_ref[z, k, d]).astype(jnp.bfloat16)
             for g in range(per_group):
-                col = (k * per_group + g) * HD
-                attended[d * new_len : (d + 1) * new_len, col : col + HD] = ratio[
+                attended[k, d * new_len : (d + 1) * new_len, g * HD : (g + 1) * HD] = ratio[
                     g * new_len : (g + 1) * new_len
                 ]
+        return carry
+
+    def product_of(k, index):
+        return jnp.dot(
+            attended[k],
+            wbuf[index, pl.ds(k * head_depth, head_depth), :],
+            preferred_element_type=jnp.float32,
+        )
+
+    for k in range(kv_count):
+        complete(k, 0)
+        if k == kv_count - 1:
+            break
+
+        def collect(index, carry):
+            if k == 0:
+                weight_copy(index).wait()
+                gathered[index] = product_of(k, index)
+            else:
+                gathered[index] += product_of(k, index)
+            return carry
+
+        lax.fori_loop(0, tiles, collect, 0)
 
     def join(index):
         core_copy(index).wait_recv()
@@ -486,8 +501,11 @@
             part_copy(index, step).start()
 
     def project(index, carry):
-        weight_copy(index).wait()
-        product = jnp.dot(attended[...], wbuf[index], preferred_element_type=jnp.float32)
+        if kv_count == 1:
+            weight_copy(index).wait()
+        product = product_of(kv_count - 1, index)
+        if kv_count > 1:
+            product = product + gathered[index]
         product = product.astype(jnp.bfloat16)
         for dest in range(shards):
             part[index, dest % CORES, dest // CORES] = product[
@@ -495,14 +513,19 @@
             ]
         core_copy(index).start()
 
-        @pl.when(index > 0)
+        @pl.when(index >= LAG)
         def _():
-            join(index - 1)
+            join(index - LAG)
 
         return carry
 
     lax.fori_loop(0, tiles, project, 0)
-    join(tiles - 1)
+
+    def join_rest(index, carry):
+        join(index)
+        return carry
+
+    lax.fori_loop(max(tiles - LAG, 0), tiles, join_rest, 0)
 
     def finish(index, carry):
         total = part[index, core, chip].astype(jnp.float32) + sibling[index, chip].astype(
@@ -525,16 +548,18 @@
     lax.fori_loop(0, tiles, drain, 0)
 
     def drain_back(turn, carry):
-        back_copy(served(turn)).wait_send()
-        log_copy(served(turn)).wait_send()
+        for k in range(kv_count):
+            back_copy(served(turn), k, z).wait_send()
+            log_copy(served(turn), k, z).wait_send()
         return carry
 
     lax.fori_loop(0, outer - 1, drain_back, 0)
 
     def drain_line(group, carry):
-        for step in range(1, inner):
-            page_copy(step, group).wait_send()
         for k in range(kv_count):
+            for step in range(1, inner):
+                page_copy(step, group, k).wait_send()
+
             @pl.when((group <= z) & (z < outer - 1))
             def _():
                 q_copy(group, k, 0).wait_send()
@@ -585,25 +610,25 @@
         scratch_shapes=[
             pltpu.SMEM((groups, dialogs, entries), jnp.int32),
             pltpu.SMEM((groups, dialogs), jnp.int32),
-            pltpu.SMEM((outer, inner, SLOT, 3), jnp.int32),
+            pltpu.SMEM((outer, inner, SLOT, 2), jnp.int32),
             pltpu.VMEM((pool_size, page_rows, HD), bf16),
             pltpu.VMEM((2 * kv_count * token_rows, HD), bf16),
-            pltpu.VMEM((inner - 1, outer, SLOT, page_rows, HD), bf16),
-            pltpu.VMEM((inner - 1, outer, SLOT, page_rows, HD), bf16),
+            pltpu.VMEM((outer, kv_count, SLOT, 2, page_len, HD), bf16),
+            pltpu.VMEM((inner - 1, outer, kv_count, SLOT, 2, page_len, HD), bf16),
+            pltpu.VMEM((inner - 1, outer, kv_count, SLOT, 2, page_len, HD), bf16),
             pltpu.VMEM((tiles, depth, tile), bf16),
             pltpu.VMEM((block, block), bf16),
             pltpu.VMEM((outer, kv_count, dialogs, rows, HD), bf16),
-            pltpu.VMEM((kv_count, dialogs, rows, HD), bf16),
-            pltpu.VMEM((kv_count, SLOT * page_len, HD), bf16),
-            pltpu.VMEM((kv_count, SLOT * page_len, HD), bf16),
+            pltpu.VMEM((dialogs, rows, HD), bf16),
             pltpu.VMEM((outer, kv_count, dialogs, rows, HD), f32),
             pltpu.VMEM((outer, kv_count, dialogs, rows, HD), f32),
             pltpu.VMEM((outer, kv_count, dialogs, rows, HD), f32),
             pltpu.VMEM((outer, kv_count, dialogs, rows, HD), bf16),
-            pltpu.VMEM((outer, kv_count * dialogs, rows), f32),
+            pltpu.VMEM((outer, kv_count, dialogs, rows), f32),
             pltpu.VMEM((outer, kv_count, dialogs, rows, HD), bf16),
-            pltpu.VMEM((outer, kv_count * dialogs, rows), f32),
-            pltpu.VMEM((token_rows, depth), bf16),
+            pltpu.VMEM((outer, kv_count, dialogs, rows), f32),
+            pltpu.VMEM((kv_count, token_rows, depth // kv_count), bf16),
+            pltpu.VMEM((tiles, token_rows, tile), f32),
             pltpu.VMEM((tiles, CORES, chips, block_rows, tile), bf16),
             pltpu.VMEM((tiles, chips, block_rows, tile), bf16),
             pltpu.VMEM((tiles, chips - 1, block_rows, tile), bf16),
@@ -617,12 +642,12 @@
             dma((groups,)),
             dma((2, outer, kv_count)),
             dma((outer, kv_count)),
-            dma((inner - 1, outer)),
-            dma((inner - 1, outer)),
-            dma((outer,)),
-            dma((outer,)),
-            dma((outer,)),
-            dma((outer,)),
+            dma((inner - 1, outer, kv_count)),
+            dma((inner - 1, outer, kv_count)),
+            dma((outer, kv_count)),
+            dma((outer, kv_count)),
+            dma((outer, kv_count)),
+            dma((outer, kv_count)),
             dma((tiles,)),
             dma((tiles,)),
             dma((tiles, chips - 1)),

time: 65.7 us -> 66.6 us (1.014)
  Pallas kernels: 63.9 us -> 64.8 us
    pallas_call x1, Pallas kernels: 63.9 us -> 64.8 us  [local(): pl.pallas_call(functools.partial(kernel, groups, shards), out_shape=jax.S...]
where the time goes in v2:
time: 66.6 us; the launch traced here: 66.5 us
  Pallas kernels  64.8 us (97%)
  local copies, waits for them, and re-layouts  1.67 us (3%)
    pallas_call x1, Pallas kernels, local(): pl.pallas_call(functools.partial(kernel, groups, shards), out_shape=jax.S...  64.8 us
    unnamed x1, local copies, waits for them, and re-layouts  1.67 us

profile of v2, /device:TPU:0, one launch (start us, length us, event | category | flops | bytes accessed | tf_op | source)
XLA Modules:
  0.0 66.5 jit_solution(14937667583076539016)
XLA Ops:
  0.0 64.8 %attend.1 = bf16[16,8192]{1,0:T(8,128)(2,1)} custom-call(bf16[64,2048]{1,0:T(8,128)(2,1)} %q_hbm.1, bf16[256,128]{1,0:T(8,128)(2,1)} %bitcast.11, bf16[24,512,128]{2,1,0:T(8,128)(2,1)} %bitcast.10, s32[2,12]{1,0:T(2,128)} %table_hbm.1, s32[2]{0:T(128)} %length_hbm.1, bf16[2048,8192]{1,0:T(8,128)(2,1)} %weight.1), custom_call_target="tpu_custom_call" | custom-call | tf_op jit(solution)/shard_map/attend/pallas_call | solution.py:605
  64.8 1.7 %copy.10 = bf16[16,8192]{1,0:T(8,128)(2,1)} copy(bf16[16,8192]{1,0:T(8,128)(2,1)} %attend.1) | data formatting | bytes 524288

commit v3 on v2

--- a/solution.py
+++ b/solution.py
@@ -11,8 +11,8 @@
 HD = 128
 PAGE = 128
 SLOT = 3
-TILE = 512
-LAG = 4
+TILE = 1024
+LAG = 2
 CORES = 2
 
 floor_value = -1e30
@@ -42,12 +42,13 @@
     groups, shards,
     q_hbm, fresh_hbm, pool_hbm, table_hbm, length_hbm, weight,
     out_ref,
-    table, length, listed, pool_ref, fresh_ref, kept, outgoing, arrived, wbuf, perm, qall, qcur,
+    table, length, listed, pool_ref, fresh_ref, kept, kept_side, outgoing, arrived, wbuf, perm,
+    qall, qside, qcur,
     peak_ref, amount_ref, summed_ref, back, back_log, came, came_log, attended, gathered,
     part, sibling, joined, landed,
     load_sem, q_load_sem, weight_sem,
-    table_send, table_recv, length_send, length_recv,
-    q_send, q_recv, page_send, page_recv,
+    row_send, row_recv, line_send, line_recv,
+    q_send, q_recv, side_send, side_recv, page_send, page_recv,
     back_send, back_recv, log_send, log_recv,
     core_send, core_recv, part_send, part_recv,
 ):
@@ -59,7 +60,7 @@
     x = me % inner
     pool_size = pool_ref.shape[0]
     _, kv_count, dialogs, rows, _ = qall.shape
-    entries = table.shape[2]
+    entries = table.shape[3]
     token_rows = q_hbm.shape[0]
     new_len = token_rows // dialogs
     per_group = rows // new_len
@@ -72,8 +73,8 @@
     core = mine % CORES
 
     loads = [
-        pltpu.make_async_copy(table_hbm, table.at[me], load_sem.at[0]),
-        pltpu.make_async_copy(length_hbm, length.at[me], load_sem.at[1]),
+        pltpu.make_async_copy(table_hbm, table.at[z, x], load_sem.at[0]),
+        pltpu.make_async_copy(length_hbm, length.at[z, x], load_sem.at[1]),
         pltpu.make_async_copy(pool_hbm, pool_ref, load_sem.at[2]),
         pltpu.make_async_copy(fresh_hbm, fresh_ref, load_sem.at[3]),
     ]
@@ -98,32 +99,73 @@
     loads[3].start()
 
     barrier = pltpu.get_barrier_semaphore()
-    for step in range(1, groups):
+    for step in range(1, inner):
         pl.semaphore_signal(
-            barrier, inc=1, device_id={"replica": lax.rem(me + step, groups)}, device_id_type=MESH
-        )
+            barrier,
+            inc=1,
+            device_id={"replica": z * inner + lax.rem(x + step, inner)},
+            device_id_type=MESH,
+        )
+
+    @pl.when(z < outer - 1)
+    def _():
+        pl.semaphore_signal(
+            barrier, inc=1, device_id={"replica": me + inner}, device_id_type=MESH
+        )
+
+    @pl.when(z > 0)
+    def _():
+        pl.semaphore_signal(
+            barrier, inc=1, device_id={"replica": me - inner}, device_id_type=MESH
+        )
+
     for step in range(1, shards):
         pl.semaphore_signal(
             barrier, inc=1, device_id={"tensor": lax.rem(mine + step, shards)}, device_id_type=MESH
         )
 
-    def table_copy(step):
+    def row_copies(step):
+        return [
+            pltpu.make_async_remote_copy(
+                src_ref=ref.at[z, x],
+                dst_ref=ref.at[z, x],
+                send_sem=row_send.at[which, step - 1],
+                recv_sem=row_recv.at[which, step - 1],
+                device_id={"replica": z * inner + lax.rem(x + step, inner)},
+                device_id_type=MESH,
+            )
+            for which, ref in enumerate((table, length))
+        ]
+
+    def line_copies(group, way):
+        dest = z + (1 if way == 0 else -1)
+        return [
+            pltpu.make_async_remote_copy(
+                src_ref=ref.at[group],
+                dst_ref=ref.at[group],
+                send_sem=line_send.at[which, way, group],
+                recv_sem=line_recv.at[which, group],
+                device_id={"replica": dest * inner + x},
+                device_id_type=MESH,
+            )
+            for which, ref in enumerate((table, length))
+        ]
+
+    def start(copies):
+        for copy in copies:
+            copy.start()
+
+    def wait_recv(copies):
+        for copy in copies:
+            copy.wait_recv()
+
+    def side_q_copy(step, k):
         return pltpu.make_async_remote_copy(
-            src_ref=table.at[me],
-            dst_ref=table.at[me],
-            send_sem=table_send.at[step],
-            recv_sem=table_recv.at[step],
-            device_id={"replica": lax.rem(me + step, groups)},
-            device_id_type=MESH,
-        )
-
-    def length_copy(step):
-        return pltpu.make_async_remote_copy(
-            src_ref=length.at[me],
-            dst_ref=length.at[me],
-            send_sem=length_send.at[step],
-            recv_sem=length_recv.at[step],
-            device_id={"replica": lax.rem(me + step, groups)},
+            src_ref=qall.at[z, k],
+            dst_ref=qside.at[step - 1, k],
+            send_sem=side_send.at[step - 1, k],
+            recv_sem=side_recv.at[step - 1, k],
+            device_id={"replica": z * inner + lax.rem(x + step, inner)},
             device_id_type=MESH,
         )
 
@@ -168,6 +210,22 @@
             device_id_type=MESH,
         )
 
+    def side_copies(step, k):
+        return [
+            pltpu.make_async_remote_copy(
+                src_ref=src.at[outer + step - 1, k],
+                dst_ref=dst.at[outer + step - 1, k],
+                send_sem=sends.at[outer + step - 1, k],
+                recv_sem=recvs.at[outer + step - 1, k],
+                device_id={"replica": z * inner + lax.rem(x - step + inner, inner)},
+                device_id_type=MESH,
+            )
+            for src, dst, sends, recvs in (
+                (back, came, back_send, back_recv),
+                (back_log, came_log, log_send, log_recv),
+            )
+        ]
+
     def weight_copy(index):
         return pltpu.make_async_copy(
             weight.at[:, pl.ds(pl.multiple_of(index * tile, tile), tile)],
@@ -208,10 +266,10 @@
 
     loads[0].wait()
     loads[1].wait()
-    pl.semaphore_wait(barrier, groups + shards - 2)
-    for step in range(1, groups):
-        table_copy(step).start()
-        length_copy(step).start()
+    beside_line = (z > 0).astype(jnp.int32) + (z < outer - 1).astype(jnp.int32)
+    pl.semaphore_wait(barrier, inner - 1 + shards - 1 + beside_line)
+    for step in range(1, inner):
+        start(row_copies(step))
     for copy in q_loads:
         copy.wait()
     for k in range(kv_count):
@@ -222,6 +280,20 @@
         @pl.when(z > 0)
         def _():
             q_copy(z, k, 1).start()
+
+        for step in range(1, inner):
+            side_q_copy(step, k).start()
+
+    for step in range(1, inner):
+        wait_recv(row_copies(step))
+
+    @pl.when(z < outer - 1)
+    def _():
+        start(line_copies(z, 0))
+
+    @pl.when(z > 0)
+    def _():
+        start(line_copies(z, 1))
 
     loads[2].wait()
     loads[3].wait()
@@ -232,9 +304,9 @@
         shelf, dialog, fill = [zero] * SLOT, [zero] * SLOT, [zero] * SLOT
         low = owner * pool_size
         for d in range(dialogs):
-            total = length[group, d]
+            total = length[group // inner, group % inner, d]
             for e in range(entries):
-                place = table[group, d, e] - low
+                place = table[group // inner, group % inner, d, e] - low
                 live = jnp.minimum(total - e * PAGE, PAGE)
                 hit = (place >= 0) & (place < pool_size) & (live > 0)
                 for s in range(SLOT):
@@ -245,15 +317,22 @@
                 count = count + hit.astype(jnp.int32)
         return shelf, dialog, fill
 
-    def await_tables(group):
-        for other in range(inner):
-            source = group * inner + other
-            step = lax.rem(me - source + groups, groups)
-
-            @pl.when(source != me)
-            def _():
-                table_copy(step).wait_recv()
-                length_copy(step).wait_recv()
+    def relay_tables(distance):
+        @pl.when(z >= distance)
+        def _():
+            wait_recv(line_copies(z - distance, 0))
+
+        @pl.when((z >= distance) & (z < outer - 1))
+        def _():
+            start(line_copies(z - distance, 0))
+
+        @pl.when(z < outer - distance)
+        def _():
+            wait_recv(line_copies(z + distance, 1))
+
+        @pl.when((z < outer - distance) & (z > 0))
+        def _():
+            start(line_copies(z + distance, 1))
 
     def separate(shelf, put):
         for s in range(SLOT):
@@ -268,9 +347,25 @@
                         low = (2 * k + kind) * block_tokens
                         put(k, s, kind, b * block_tokens, split[low : low + block_tokens])
 
+    def relay(distance, k):
+        @pl.when(z >= distance)
+        def _():
+            q_copy(z - distance, k, 0).wait_recv()
+
+        @pl.when((z >= distance) & (z < outer - 1))
+        def _():
+            q_copy(z - distance, k, 0).start()
+
+        @pl.when(z < outer - distance)
+        def _():
+            q_copy(z + distance, k, 1).wait_recv()
+
+        @pl.when((z < outer - distance) & (z > 0))
+        def _():
+            q_copy(z + distance, k, 1).start()
+
     def send_pages(turn, carry):
         group = served(turn)
-        await_tables(group)
         for step in range(1, inner):
             shelf, _, _ = request(group * inner + lax.rem(x + step, inner), me)
 
@@ -282,19 +377,33 @@
                 page_copy(step, group, k).start()
         return carry
 
-    lax.fori_loop(0, outer, send_pages, 0)
+    for distance in range(1, half + 1):
+        relay_tables(distance)
+        if distance < half:
+            relay(distance, 0)
+    lax.fori_loop(0, 1, send_pages, 0)
+    for k in range(1, kv_count):
+        for distance in range(1, half):
+            relay(distance, k)
+    for distance in range(half + 1, outer):
+        relay_tables(distance)
+    lax.fori_loop(1, outer - 1, send_pages, 0)
 
     for index in range(tiles):
         weight_copy(index).start()
 
     def list_pages(group, carry):
         for step in range(inner):
+            behind = lax.rem(x - step + inner, inner)
+            own_row = (group == z).astype(jnp.int32)
             shelf, dialog, fill = request(
-                group * inner + x, z * inner + lax.rem(x - step + inner, inner)
+                group * inner + own_row * behind + (1 - own_row) * x,
+                z * inner + own_row * x + (1 - own_row) * behind,
             )
             for s in range(SLOT):
                 listed[group, step, s, 0] = dialog[s]
                 listed[group, step, s, 1] = fill[s]
+                listed[group, step, s, 2] = shelf[s]
             if step == 0:
 
                 def put(k, s, kind, at, rows_of):
@@ -303,7 +412,15 @@
                 separate(shelf, put)
         return carry
 
-    lax.fori_loop(0, outer, list_pages, 0)
+    lax.fori_loop(0, half, list_pages, 0)
+    relay(half, 0)
+    lax.fori_loop(half, outer, list_pages, 0)
+    for step in range(1, inner):
+
+        def put_side(k, s, kind, at, rows_of):
+            kept_side[step - 1, k, s, kind, at : at + block_tokens, :] = rows_of
+
+        separate([listed[z, step, s, 2] for s in range(SLOT)], put_side)
 
     fresh_rows = fresh_ref.shape[0]
     split = jnp.dot(
@@ -328,16 +445,19 @@
             )
             summed_ref[z, k, d] = jnp.dot(weights, values, preferred_element_type=jnp.float32)
 
-    def absorb(group, k, step, pages, first):
+    for k in range(1, kv_count):
+        relay(half, k)
+
+    def absorb(group, k, q_ref, listing, pages, first):
         position = lax.broadcasted_iota(jnp.int32, (rows, PAGE), 1)
-        dialog = [listed[group, step, s, 0] for s in range(SLOT)]
-        fill = [listed[group, step, s, 1] for s in range(SLOT)]
+        dialog = [listing[s, 0] for s in range(SLOT)]
+        fill = [listing[s, 1] for s in range(SLOT)]
         owned = [
             [jnp.broadcast_to(dialog[s], (rows, HD)) == d for d in range(dialogs)]
             for s in range(SLOT)
         ]
         for d in range(dialogs):
-            qcur[d] = qall[group, k, d]
+            qcur[d] = q_ref[k, d]
         scores, highs = [], []
         for s in range(SLOT):
             found = lax.dot_general(
@@ -384,12 +504,19 @@
             summed_ref[group, k, d] = total
 
     def absorb_kept(group, k, first):
-        absorb(group, k, 0, kept.at[group, k], first)
+        absorb(group, k, qall.at[group], listed.at[group, 0], kept.at[group, k], first)
 
     def absorb_arrived(group, k):
         for step in range(1, inner):
             page_copy(step, group, k).wait_recv()
-            absorb(group, k, step, arrived.at[step - 1, group, k], False)
+            absorb(
+                group,
+                k,
+                qall.at[group],
+                listed.at[group, step],
+                arrived.at[step - 1, group, k],
+                False,
+            )
 
     def begin(k, carry):
         absorb_kept(z, k, False)
@@ -397,49 +524,57 @@
 
     lax.fori_loop(0, kv_count, begin, 0)
 
-    def relay(distance):
-        for k in range(kv_count):
-            @pl.when(z >= distance)
-            def _():
-                q_copy(z - distance, k, 0).wait_recv()
-
-            @pl.when((z >= distance) & (z < outer - 1))
-            def _():
-                q_copy(z - distance, k, 0).start()
-
-            @pl.when(z < outer - distance)
-            def _():
-                q_copy(z + distance, k, 1).wait_recv()
-
-            @pl.when((z < outer - distance) & (z > 0))
-            def _():
-                q_copy(z + distance, k, 1).start()
+    def pack(slot, k):
+        for d in range(dialogs):
+            amount = jnp.maximum(amount_ref[slot, k, d], tiny_value)
+            back[slot, k, d] = (summed_ref[slot, k, d] / amount).astype(jnp.bfloat16)
+            log = peak_ref[slot, k, d] + jnp.log2(amount)
+            back_log[slot, k, d : d + 1, :] = jnp.transpose(log)[:1]
 
     def serve(index, carry):
         group = served(index // kv_count)
         k = index % kv_count
         absorb_kept(group, k, True)
         absorb_arrived(group, k)
-        for d in range(dialogs):
-            amount = jnp.maximum(amount_ref[group, k, d], tiny_value)
-            back[group, k, d] = (summed_ref[group, k, d] / amount).astype(jnp.bfloat16)
-            log = peak_ref[group, k, d] + jnp.log2(amount)
-            back_log[group, k, d : d + 1, :] = jnp.transpose(log)[:1]
+        pack(group, k)
         back_copy(group, k, z).start()
         log_copy(group, k, z).start()
         return carry
 
-    for distance in range(1, half + 1):
-        relay(distance)
-    lax.fori_loop(0, kv_count, serve, 0)
-    for distance in range(half + 1, outer):
-        relay(distance)
-    lax.fori_loop(kv_count, (outer - 1) * kv_count, serve, 0)
+    def serve_then_relay(index, carry):
+        serve(index, 0)
+        relay(half + 1 + index // kv_count, index % kv_count)
+        return carry
+
+    def serve_row(k, carry):
+        for step in range(1, inner):
+            side_q_copy(step, k).wait_recv()
+            slot = outer + step - 1
+            absorb(
+                slot,
+                k,
+                qside.at[step - 1],
+                listed.at[z, step],
+                kept_side.at[step - 1, k],
+                True,
+            )
+            pack(slot, k)
+            start(side_copies(step, k))
+        return carry
+
+    lax.fori_loop(0, kv_count, serve_then_relay, 0)
+    lax.fori_loop(0, kv_count, serve_row, 0)
+    lax.fori_loop(kv_count, (half - 1) * kv_count, serve_then_relay, 0)
+    lax.fori_loop((half - 1) * kv_count, (outer - 1) * kv_count, serve, 0)
 
     def merge(turn, k):
         source = served(turn)
         back_copy(source, k, source).wait_recv()
         log_copy(source, k, source).wait_recv()
+        merge_slot(source, k)
+        return k
+
+    def merge_slot(source, k):
         for d in range(dialogs):
             line = came_log[source, k, d : d + 1, :]
             log = jnp.transpose(jnp.broadcast_to(line, (HD, rows)))
@@ -452,14 +587,15 @@
             summed_ref[z, k, d] = keep * summed_ref[z, k, d] + take * came[
                 source, k, d
             ].astype(jnp.float32)
-        return k
 
     head_depth = per_group * HD
 
     def complete(k, carry):
         lax.fori_loop(0, half, merge, k)
-        absorb_arrived(z, k)
         lax.fori_loop(half, outer - 1, merge, k)
+        for step in range(1, inner):
+            wait_recv(side_copies(step, k))
+            merge_slot(outer + step - 1, k)
         for d in range(dialogs):
             ratio = (summed_ref[z, k, d] / amount_ref[z, k, d]).astype(jnp.bfloat16)
             for g in range(per_group):
@@ -557,9 +693,6 @@
 
     def drain_line(group, carry):
         for k in range(kv_count):
-            for step in range(1, inner):
-                page_copy(step, group, k).wait_send()
-
             @pl.when((group <= z) & (z < outer - 1))
             def _():
                 q_copy(group, k, 0).wait_send()
@@ -568,12 +701,31 @@
             def _():
                 q_copy(group, k, 1).wait_send()
 
+            @pl.when(group != z)
+            def _():
+                for step in range(1, inner):
+                    page_copy(step, group, k).wait_send()
+
+        @pl.when((group <= z) & (z < outer - 1))
+        def _():
+            for copy in line_copies(group, 0):
+                copy.wait_send()
+
+        @pl.when((group >= z) & (z > 0))
+        def _():
+            for copy in line_copies(group, 1):
+                copy.wait_send()
+
         return carry
 
     lax.fori_loop(0, outer, drain_line, 0)
-    for step in range(1, groups):
-        table_copy(step).wait_send()
-        length_copy(step).wait_send()
+    for step in range(1, inner):
+        for copy in row_copies(step):
+            copy.wait_send()
+        for k in range(kv_count):
+            side_q_copy(step, k).wait_send()
+            for copy in side_copies(step, k):
+                copy.wait_send()
 
 
 def local(queries, kv_new, pool, page_table, hist_len, o_weight):
@@ -593,6 +745,7 @@
     block_rows = token_rows // shards
     chips = shards // CORES
     page_rows = 2 * kv_count * page_len
+    slots = outer + inner - 1
     block = 256
     pages = pool.reshape(pool_size, page_len, 2, kv_count, HD).transpose(0, 1, 3, 2, 4)
     pages = pages.reshape(pool_size, page_rows, HD)
@@ -608,25 +761,27 @@
         in_specs=[anywhere] * 6,
         out_specs=vmem,
         scratch_shapes=[
-            pltpu.SMEM((groups, dialogs, entries), jnp.int32),
-            pltpu.SMEM((groups, dialogs), jnp.int32),
-            pltpu.SMEM((outer, inner, SLOT, 2), jnp.int32),
+            pltpu.SMEM((outer, inner, dialogs, entries), jnp.int32),
+            pltpu.SMEM((outer, inner, dialogs), jnp.int32),
+            pltpu.SMEM((outer, inner, SLOT, 3), jnp.int32),
             pltpu.VMEM((pool_size, page_rows, HD), bf16),
             pltpu.VMEM((2 * kv_count * token_rows, HD), bf16),
             pltpu.VMEM((outer, kv_count, SLOT, 2, page_len, HD), bf16),
+            pltpu.VMEM((inner - 1, kv_count, SLOT, 2, page_len, HD), bf16),
             pltpu.VMEM((inner - 1, outer, kv_count, SLOT, 2, page_len, HD), bf16),
             pltpu.VMEM((inner - 1, outer, kv_count, SLOT, 2, page_len, HD), bf16),
             pltpu.VMEM((tiles, depth, tile), bf16),
             pltpu.VMEM((block, block), bf16),
             pltpu.VMEM((outer, kv_count, dialogs, rows, HD), bf16),
+            pltpu.VMEM((inner - 1, kv_count, dialogs, rows, HD), bf16),
             pltpu.VMEM((dialogs, rows, HD), bf16),
-            pltpu.VMEM((outer, kv_count, dialogs, rows, HD), f32),
-            pltpu.VMEM((outer, kv_count, dialogs, rows, HD), f32),
-            pltpu.VMEM((outer, kv_count, dialogs, rows, HD), f32),
-            pltpu.VMEM((outer, kv_count, dialogs, rows, HD), bf16),
-            pltpu.VMEM((outer, kv_count, dialogs, rows), f32),
-            pltpu.VMEM((outer, kv_count, dialogs, rows, HD), bf16),
-            pltpu.VMEM((outer, kv_count, dialogs, rows), f32),
+            pltpu.VMEM((slots, kv_count, dialogs, rows, HD), f32),
+            pltpu.VMEM((slots, kv_count, dialogs, rows, HD), f32),
+            pltpu.VMEM((slots, kv_count, dialogs, rows, HD), f32),
+            pltpu.VMEM((slots, kv_count, dialogs, rows, HD), bf16),
+            pltpu.VMEM((slots, kv_count, dialogs, rows), f32),
+            pltpu.VMEM((slots, kv_count, dialogs, rows, HD), bf16),
+            pltpu.VMEM((slots, kv_count, dialogs, rows), f32),
             pltpu.VMEM((kv_count, token_rows, depth // kv_count), bf16),
             pltpu.VMEM((tiles, token_rows, tile), f32),
             pltpu.VMEM((tiles, CORES, chips, block_rows, tile), bf16),
@@ -636,18 +791,20 @@
             dma((4,)),
             dma((kv_count, dialogs, per_group)),
             dma((tiles,)),
-            dma((groups,)),
-            dma((groups,)),
-            dma((groups,)),
-            dma((groups,)),
+            dma((2, inner - 1)),
+            dma((2, inner - 1)),
+            dma((2, 2, outer)),
+            dma((2, outer)),
             dma((2, outer, kv_count)),
             dma((outer, kv_count)),
+            dma((inner - 1, kv_count)),
+            dma((inner - 1, kv_count)),
             dma((inner - 1, outer, kv_count)),
             dma((inner - 1, outer, kv_count)),
-            dma((outer, kv_count)),
-            dma((outer, kv_count)),
-            dma((outer, kv_count)),
-            dma((outer, kv_count)),
+            dma((slots, kv_count)),
+            dma((slots, kv_count)),
+            dma((slots, kv_count)),
+            dma((slots, kv_count)),
             dma((tiles,)),
             dma((tiles,)),
             dma((tiles, chips - 1)),

time: 66.6 us -> 66.4 us (level)
  no operation moved by 1% of the time
where the time goes in v3:
time: 66.4 us; the launch traced here: 66.3 us
  Pallas kernels  64.6 us (97%)
  local copies, waits for them, and re-layouts  1.67 us (3%)
    pallas_call x1, Pallas kernels, local(): pl.pallas_call(functools.partial(kernel, groups, shards), out_shape=jax.S...  64.6 us
    unnamed x1, local copies, waits for them, and re-layouts  1.67 us

profile of v3, /device:TPU:0, one launch (start us, length us, event | category | flops | bytes accessed | tf_op | source)
XLA Modules:
  0.0 66.3 jit_solution(12099053375723252814)
XLA Ops:
  0.0 64.6 %attend.1 = bf16[16,8192]{1,0:T(8,128)(2,1)} custom-call(bf16[64,2048]{1,0:T(8,128)(2,1)} %q_hbm.1, bf16[256,128]{1,0:T(8,128)(2,1)} %bitcast.11, bf16[24,512,128]{2,1,0:T(8,128)(2,1)} %bitcast.10, s32[2,12]{1,0:T(2,128)} %table_hbm.1, s32[2]{0:T(128)} %length_hbm.1, bf16[2048,8192]{1,0:T(8,128)(2,1)} %weight.1), custom_call_target="tpu_custom_call" | custom-call | tf_op jit(solution)/shard_map/attend/pallas_call | solution.py:758
  64.6 1.7 %copy.10 = bf16[16,8192]{1,0:T(8,128)(2,1)} copy(bf16[16,8192]{1,0:T(8,128)(2,1)} %attend.1) | data formatting | bytes 524288

commit v4 on v2

--- a/solution.py
+++ b/solution.py
@@ -11,8 +11,8 @@
 HD = 128
 PAGE = 128
 SLOT = 3
-TILE = 512
-LAG = 4
+TILE = 1024
+LAG = 2
 CORES = 2
 
 floor_value = -1e30
@@ -268,6 +268,23 @@
                         low = (2 * k + kind) * block_tokens
                         put(k, s, kind, b * block_tokens, split[low : low + block_tokens])
 
+    def relay(distance, k):
+        @pl.when(z >= distance)
+        def _():
+            q_copy(z - distance, k, 0).wait_recv()
+
+        @pl.when((z >= distance) & (z < outer - 1))
+        def _():
+            q_copy(z - distance, k, 0).start()
+
+        @pl.when(z < outer - distance)
+        def _():
+            q_copy(z + distance, k, 1).wait_recv()
+
+        @pl.when((z < outer - distance) & (z > 0))
+        def _():
+            q_copy(z + distance, k, 1).start()
+
     def send_pages(turn, carry):
         group = served(turn)
         await_tables(group)
@@ -282,7 +299,10 @@
                 page_copy(step, group, k).start()
         return carry
 
-    lax.fori_loop(0, outer, send_pages, 0)
+    lax.fori_loop(0, 1, send_pages, 0)
+    for distance in range(1, half):
+        relay(distance, 0)
+    lax.fori_loop(1, outer, send_pages, 0)
 
     for index in range(tiles):
         weight_copy(index).start()
@@ -303,7 +323,11 @@
                 separate(shelf, put)
         return carry
 
-    lax.fori_loop(0, outer, list_pages, 0)
+    lax.fori_loop(0, half, list_pages, 0)
+    for k in range(1, kv_count):
+        for distance in range(1, half):
+            relay(distance, k)
+    lax.fori_loop(half, outer, list_pages, 0)
 
     fresh_rows = fresh_ref.shape[0]
     split = jnp.dot(
@@ -397,24 +421,6 @@
 
     lax.fori_loop(0, kv_count, begin, 0)
 
-    def relay(distance):
-        for k in range(kv_count):
-            @pl.when(z >= distance)
-            def _():
-                q_copy(z - distance, k, 0).wait_recv()
-
-            @pl.when((z >= distance) & (z < outer - 1))
-            def _():
-                q_copy(z - distance, k, 0).start()
-
-            @pl.when(z < outer - distance)
-            def _():
-                q_copy(z + distance, k, 1).wait_recv()
-
-            @pl.when((z < outer - distance) & (z > 0))
-            def _():
-                q_copy(z + distance, k, 1).start()
-
     def serve(index, carry):
         group = served(index // kv_count)
         k = index % kv_count
@@ -429,12 +435,12 @@
         log_copy(group, k, z).start()
         return carry
 
-    for distance in range(1, half + 1):
-        relay(distance)
-    lax.fori_loop(0, kv_count, serve, 0)
-    for distance in range(half + 1, outer):
-        relay(distance)
-    lax.fori_loop(kv_count, (outer - 1) * kv_count, serve, 0)
+    def serve_far(index, carry):
+        relay(half + index // kv_count, index % kv_count)
+        return serve(index, carry)
+
+    lax.fori_loop(0, half * kv_count, serve_far, 0)
+    lax.fori_loop(half * kv_count, (outer - 1) * kv_count, serve, 0)
 
     def merge(turn, k):
         source = served(turn)

time: 66.6 us -> 63.2 us (0.949)
  Pallas kernels: 64.8 us -> 61.4 us
    pallas_call x1, Pallas kernels: 64.8 us -> 61.4 us  [local(): pl.pallas_call(functools.partial(kernel, groups, shards), out_shape=jax.S...]
where the time goes in v4:
time: 63.2 us; the launch traced here: 63.1 us
  Pallas kernels  61.4 us (97%)
  local copies, waits for them, and re-layouts  1.67 us (3%)
    pallas_call x1, Pallas kernels, local(): pl.pallas_call(functools.partial(kernel, groups, shards), out_shape=jax.S...  61.4 us
    unnamed x1, local copies, waits for them, and re-layouts  1.67 us

profile of v4, /device:TPU:0, one launch (start us, length us, event | category | flops | bytes accessed | tf_op | source)
XLA Modules:
  0.0 63.1 jit_solution(1369648547300985423)
XLA Ops:
  0.0 61.4 %attend.1 = bf16[16,8192]{1,0:T(8,128)(2,1)} custom-call(bf16[64,2048]{1,0:T(8,128)(2,1)} %q_hbm.1, bf16[256,128]{1,0:T(8,128)(2,1)} %bitcast.11, bf16[24,512,128]{2,1,0:T(8,128)(2,1)} %bitcast.10, s32[2,12]{1,0:T(2,128)} %table_hbm.1, s32[2]{0:T(128)} %length_hbm.1, bf16[2048,8192]{1,0:T(8,128)(2,1)} %weight.1), custom_call_target="tpu_custom_call" | custom-call | tf_op jit(solution)/shard_map/attend/pallas_call | solution.py:611
  61.4 1.7 %copy.10 = bf16[16,8192]{1,0:T(8,128)(2,1)} copy(bf16[16,8192]{1,0:T(8,128)(2,1)} %attend.1) | data formatting | bytes 524288

commit v5 on v4

--- a/solution.py
+++ b/solution.py
@@ -11,9 +11,11 @@
 HD = 128
 PAGE = 128
 SLOT = 3
-TILE = 1024
-LAG = 2
+TILE = 2048
+LAG = 1
 CORES = 2
+
+BATCH = 2
 
 floor_value = -1e30
 tiny_value = 1e-30
@@ -461,6 +463,7 @@
         return k
 
     head_depth = per_group * HD
+    batch = math.gcd(tiles, BATCH)
 
     def complete(k, carry):
         lax.fori_loop(0, half, merge, k)
@@ -486,15 +489,17 @@
         if k == kv_count - 1:
             break
 
-        def collect(index, carry):
-            if k == 0:
-                weight_copy(index).wait()
-                gathered[index] = product_of(k, index)
-            else:
-                gathered[index] += product_of(k, index)
+        def collect(turn, carry):
+            for offset in range(batch):
+                index = turn * batch + offset
+                if k == 0:
+                    weight_copy(index).wait()
+                    gathered[index] = product_of(k, index)
+                else:
+                    gathered[index] += product_of(k, index)
             return carry
 
-        lax.fori_loop(0, tiles, collect, 0)
+        lax.fori_loop(0, tiles // batch, collect, 0)
 
     def join(index):
         core_copy(index).wait_recv()

time: 63.2 us -> 62.9 us (level)
  no operation moved by 1% of the time
where the time goes in v5:
time: 62.9 us; the launch traced here: 62.8 us
  Pallas kernels  61.1 us (97%)
  local copies, waits for them, and re-layouts  1.67 us (3%)
    pallas_call x1, Pallas kernels, local(): pl.pallas_call(functools.partial(kernel, groups, shards), out_shape=jax.S...  61.1 us
    unnamed x1, local copies, waits for them, and re-layouts  1.67 us

profile of v5, /device:TPU:0, one launch (start us, length us, event | category | flops | bytes accessed | tf_op | source)
XLA Modules:
  0.0 62.8 jit_solution(15626709376873509925)
XLA Ops:
  0.0 61.1 %attend.1 = bf16[16,8192]{1,0:T(8,128)(2,1)} custom-call(bf16[64,2048]{1,0:T(8,128)(2,1)} %q_hbm.1, bf16[256,128]{1,0:T(8,128)(2,1)} %bitcast.11, bf16[24,512,128]{2,1,0:T(8,128)(2,1)} %bitcast.10, s32[2,12]{1,0:T(2,128)} %table_hbm.1, s32[2]{0:T(128)} %length_hbm.1, bf16[2048,8192]{1,0:T(8,128)(2,1)} %weight.1), custom_call_target="tpu_custom_call" | custom-call | tf_op jit(solution)/shard_map/attend/pallas_call | solution.py:616
  61.1 1.7 %copy.10 = bf16[16,8192]{1,0:T(8,128)(2,1)} copy(bf16[16,8192]{1,0:T(8,128)(2,1)} %attend.1) | data formatting | bytes 524288

commit v6 on v5

--- a/solution.py
+++ b/solution.py
@@ -46,8 +46,8 @@
     out_ref,
     table, length, listed, pool_ref, fresh_ref, kept, outgoing, arrived, wbuf, perm, qall, qcur,
     peak_ref, amount_ref, summed_ref, back, back_log, came, came_log, attended, gathered,
-    part, sibling, joined, landed,
-    load_sem, q_load_sem, weight_sem,
+    part, sibling, joined, landed, result,
+    load_sem, q_load_sem, weight_sem, out_sem,
     table_send, table_recv, length_send, length_recv,
     q_send, q_recv, page_send, page_recv,
     back_send, back_recv, log_send, log_recv,
@@ -211,7 +211,7 @@
     loads[0].wait()
     loads[1].wait()
     pl.semaphore_wait(barrier, groups + shards - 2)
-    for step in range(1, groups):
+    for step in sorted(range(1, groups), key=lambda d: -min(d, groups - d)):
         table_copy(step).start()
         length_copy(step).start()
     for copy in q_loads:
@@ -538,6 +538,13 @@
 
     lax.fori_loop(max(tiles - LAG, 0), tiles, join_rest, 0)
 
+    def out_copy(index):
+        return pltpu.make_async_copy(
+            result.at[index],
+            out_ref.at[:, pl.ds(pl.multiple_of(index * tile, tile), tile)],
+            out_sem.at[index],
+        )
+
     def finish(index, carry):
         total = part[index, core, chip].astype(jnp.float32) + sibling[index, chip].astype(
             jnp.float32
@@ -545,12 +552,14 @@
         for step in range(1, chips):
             part_copy(index, step).wait_recv()
             total = total + landed[index, step - 1].astype(jnp.float32)
-        out_ref[:, pl.ds(pl.multiple_of(index * tile, tile), tile)] = total.astype(out_ref.dtype)
+        result[index] = total.astype(out_ref.dtype)
+        out_copy(index).start()
         return carry
 
     lax.fori_loop(0, tiles, finish, 0)
 
     def drain(index, carry):
+        out_copy(index).wait()
         core_copy(index).wait_send()
         for step in range(1, chips):
             part_copy(index, step).wait_send()
@@ -609,7 +618,6 @@
     pages = pages.reshape(pool_size, page_rows, HD)
     fresh = kv_new.reshape(token_rows, 2, kv_count, HD).transpose(0, 2, 1, 3)
     fresh = fresh.reshape(2 * kv_count * token_rows, HD)
-    vmem = pl.BlockSpec(memory_space=pltpu.VMEM)
     anywhere = pl.BlockSpec(memory_space=pl.ANY)
     dma = pltpu.SemaphoreType.DMA
     bf16, f32 = jnp.bfloat16, jnp.float32
@@ -617,7 +625,7 @@
         functools.partial(kernel, groups, shards),
         out_shape=jax.ShapeDtypeStruct((block_rows, model), jnp.bfloat16),
         in_specs=[anywhere] * 6,
-        out_specs=vmem,
+        out_specs=anywhere,
         scratch_shapes=[
             pltpu.SMEM((groups, dialogs, entries), jnp.int32),
             pltpu.SMEM((groups, dialogs), jnp.int32),
@@ -644,8 +652,10 @@
             pltpu.VMEM((tiles, chips, block_rows, tile), bf16),
             pltpu.VMEM((tiles, chips - 1, block_rows, tile), bf16),
             pltpu.VMEM((tiles, chips - 1, block_rows, tile), bf16),
+            pltpu.VMEM((tiles, block_rows, tile), bf16),
             dma((4,)),
             dma((kv_count, dialogs, per_group)),
+            dma((tiles,)),
             dma((tiles,)),
             dma((groups,)),
             dma((groups,)),

time: 62.9 us -> 62.8 us (level)
  no operation moved by 1% of the time
where the time goes in v6:
time: 62.8 us; the launch traced here: 62.6 us
  Pallas kernels  60.9 us (97%)
  local copies, waits for them, and re-layouts  1.67 us (3%)
    pallas_call x1, Pallas kernels, local(): pl.pallas_call(functools.partial(kernel, groups, shards), out_shape=jax.S...  60.9 us
    unnamed x1, local copies, waits for them, and re-layouts  1.67 us

profile of v6, /device:TPU:0, one launch (start us, length us, event | category | flops | bytes accessed | tf_op | source)
XLA Modules:
  0.0 62.6 jit_solution(11809741237190575268)
XLA Ops:
  0.0 60.9 %attend.1 = bf16[16,8192]{1,0:T(8,128)(2,1)} custom-call(bf16[64,2048]{1,0:T(8,128)(2,1)} %q_hbm.1, bf16[256,128]{1,0:T(8,128)(2,1)} %bitcast.11, bf16[24,512,128]{2,1,0:T(8,128)(2,1)} %bitcast.10, s32[2,12]{1,0:T(2,128)} %table_hbm.1, s32[2]{0:T(128)} %length_hbm.1, bf16[2048,8192]{1,0:T(8,128)(2,1)} %weight.1), custom_call_target="tpu_custom_call" | custom-call | tf_op jit(solution)/shard_map/attend/pallas_call | solution.py:624
  61.0 1.7 %copy.10 = bf16[16,8192]{1,0:T(8,128)(2,1)} copy(bf16[16,8192]{1,0:T(8,128)(2,1)} %attend.1) | data formatting | bytes 524288
